TPU v7x, 256 devices: a whole 4x4x8 slice. The times are simulated.
256 devices in a mesh: row: 32 (over z, x_hi, core), col: 8 (over y, x_lo).
Axes of the slice: x: 4 (x_hi: 2, x_lo: 2; x = x_hi * 2 + x_lo), y: 4, z: 8, core: 2. Of those that a mesh axis runs over, the one named last changes fastest.
Arguments:
- qkv: bfloat16 [512, 64, 3, 3072], P('row', 'col'), may hold values from -6 to 6
- cotangent: bfloat16 [512, 64, 3072], P('row', 'col'), may hold values from -6 to 6
- norm_gains: float32 [2, 128], replicated, may hold values from 0.1 to 1.9
- rel_table: float32 [24, 15, 15], replicated, may hold values from -6 to 250
- shifts: int32 [2], replicated, may hold values from 1 to 7
- mask_ids: int32 [512, 64], replicated, may hold values from 0 to 2
Outputs:
- attention: bfloat16 [512, 64, 3072], P('row', 'col')
- d_qkv: bfloat16 [512, 64, 3, 3072], P('row', 'col')
- d_gains: float32 [2, 128], replicated
- d_table: float32 [24, 15, 15], replicated
All inputs are finite; a program needn't handle non-finite values.
Results may differ from a plain program's by a relative error of at most 0.0073.
Values may be sent and summed in bfloat16 or wider, within the bound.
No kernel may reach another device: no remote copies, remote signals or barrier semaphores. Data moves between devices by JAX's collectives and lax.ppermute only.
A program may use at most 192 MiB of HBM per device.

v0:
```python
import functools
import math

import jax
import jax.numpy as jnp
from jax import lax
from jax.sharding import Mesh
from jax.sharding import PartitionSpec as P

ROW = ("row_0", "row_1", "row_2")
COL = ("col_0", "col_1")
ROW_COL = ("row_0", "row_1", "row_2", "col_0", "col_1")


EPSILON = 1e-06
NEG_FILL = -1e30


def shifted(value, axis, steps):
    count = lax.axis_size(axis)
    pairs = [(source, (source + steps) % count) for source in range(count)]
    return lax.ppermute(value, axis, pairs)


def over_axes(array, axes):
    return functools.reduce(lax.psum, axes, array)


def head_norm(inputs, gain_vec):
    values = inputs.astype(jnp.float32)
    average = jnp.mean(values, axis=-1, keepdims=True)
    centred = values - average
    variance = jnp.mean(centred * centred, axis=-1, keepdims=True)
    inv_sigma = lax.rsqrt(variance + EPSILON)
    x_hat = centred * inv_sigma
    return (x_hat, inv_sigma, (x_hat * gain_vec).astype(jnp.bfloat16))


def norm_back(x_hat, inv_sigma, d_normed, gain_vec):
    d_hat = d_normed * gain_vec
    first_mean = jnp.mean(d_hat, axis=-1, keepdims=True)
    second_mean = jnp.mean(d_hat * x_hat, axis=-1, keepdims=True)
    d_input = inv_sigma * (d_hat - first_mean - x_hat * second_mean)
    d_gain = jnp.sum(d_normed * x_hat, axis=tuple(range(d_normed.ndim - 1)))
    return (d_input, d_gain)


def offset_table(window_size):
    span_count = 2 * window_size - 1
    places = jnp.arange(window_size * window_size, dtype=jnp.int32)
    row_pos = places // window_size
    col_pos = places % window_size
    code_grid = (row_pos[:, None] - row_pos[None, :] + window_size - 1) * span_count + (
        col_pos[:, None] - col_pos[None, :] + window_size - 1
    )
    codes = jnp.arange(span_count * span_count, dtype=jnp.int32)
    return (code_grid[:, :, None] == codes[None, None, :]).astype(jnp.float32)


def to_windows(field, window_size):
    row_count, col_count = (field.shape[0], field.shape[1])
    trailing = field.shape[2:]
    blocks = field.reshape(
        (row_count // window_size, window_size, col_count // window_size, window_size) + trailing
    )
    blocks = jnp.moveaxis(blocks, 2, 1)
    return blocks.reshape(
        (row_count // window_size * (col_count // window_size), window_size * window_size)
        + trailing
    )


def from_windows(blocks, window_size, row_count, col_count):
    trailing = blocks.shape[2:]
    field = blocks.reshape(
        (row_count // window_size, col_count // window_size, window_size, window_size) + trailing
    )
    field = jnp.moveaxis(field, 1, 2)
    return field.reshape((row_count, col_count) + trailing)


def window_core(q_norm, k_norm, values, grads, pos_bias, allowed, score_scale):
    scores = (
        jnp.einsum("wqhd,wkhd->whqk", q_norm, k_norm, preferred_element_type=jnp.float32)
        * score_scale
        + pos_bias[None]
    )
    scores = jnp.where(allowed[:, None], scores, NEG_FILL)
    row_max = jnp.max(scores, axis=-1, keepdims=True)
    weights = jnp.exp(scores - row_max)
    probs = weights / jnp.sum(weights, axis=-1, keepdims=True)
    probs_b = probs.astype(jnp.bfloat16)
    output = jnp.einsum("whqk,wkhd->wqhd", probs_b, values, preferred_element_type=jnp.float32)
    d_probs = jnp.einsum("wqhd,wkhd->whqk", grads, values, preferred_element_type=jnp.float32)
    row_dot = jnp.sum(probs * d_probs, axis=-1, keepdims=True)
    d_scores = probs * (d_probs - row_dot)
    d_scores_b = d_scores.astype(jnp.bfloat16)
    d_qnorm = (
        jnp.einsum("whqk,wkhd->wqhd", d_scores_b, k_norm, preferred_element_type=jnp.float32)
        * score_scale
    )
    d_knorm = (
        jnp.einsum("whqk,wqhd->wkhd", d_scores_b, q_norm, preferred_element_type=jnp.float32)
        * score_scale
    )
    d_value = jnp.einsum("whqk,wqhd->wkhd", probs_b, grads, preferred_element_type=jnp.float32)
    return (output, d_qnorm, d_knorm, d_value, jnp.sum(d_scores, axis=0))


def label_pairs(labels, window_size):
    label_win = to_windows(labels, window_size)
    return label_win[:, :, None] == label_win[:, None, :]


def local(qkv, cotangent, norm_gains, rel_table, shifts, mask_ids):
    tile_rows, tile_cols = (qkv.shape[0], qkv.shape[1])
    feature_width = qkv.shape[3]
    head_count = rel_table.shape[0]
    head_dim = feature_width // head_count
    span_count = rel_table.shape[1]
    window_size = (span_count + 1) // 2
    score_scale = 1.0 / math.sqrt(head_dim)
    shift_row = shifts[0]
    shift_col = shifts[1]
    grid_row = lax.axis_index(ROW) * tile_rows
    grid_col = lax.axis_index(COL) * tile_cols
    one_hot = offset_table(window_size)
    pos_bias = jnp.einsum(
        "hc,qkc->hqk",
        rel_table.reshape(head_count, span_count * span_count),
        one_hot,
        precision=lax.Precision.HIGHEST,
    )
    gain_q = norm_gains[0]
    gain_k = norm_gains[1]
    stacked = jnp.concatenate([qkv, cotangent[:, :, None]], axis=2)
    received = shifted(stacked[:window_size], ROW, -1)
    rolled = lax.dynamic_slice_in_dim(
        jnp.concatenate([stacked, received], axis=0), shift_row, tile_rows, 0
    )
    received = shifted(rolled, COL, -1)
    rolled = lax.dynamic_slice_in_dim(
        jnp.concatenate([rolled, received], axis=1), shift_col, tile_cols, 1
    )
    fields = rolled.reshape(tile_rows, tile_cols, 4, head_count, head_dim)
    q_hat, q_inv, q_norm = head_norm(fields[:, :, 0], gain_q)
    k_hat, k_inv, k_norm = head_norm(fields[:, :, 1], gain_k)
    labels = jnp.roll(mask_ids, (-(grid_row + shift_row), -(grid_col + shift_col)), (0, 1))[
        :tile_rows, :tile_cols
    ]
    output, d_qnorm, d_knorm, d_value, d_bias = window_core(
        to_windows(q_norm, window_size),
        to_windows(k_norm, window_size),
        to_windows(fields[:, :, 2], window_size),
        to_windows(fields[:, :, 3], window_size),
        pos_bias,
        label_pairs(labels, window_size),
        score_scale,
    )
    output = from_windows(output, window_size, tile_rows, tile_cols)
    d_qnorm = from_windows(d_qnorm, window_size, tile_rows, tile_cols)
    d_knorm = from_windows(d_knorm, window_size, tile_rows, tile_cols)
    d_value = from_windows(d_value, window_size, tile_rows, tile_cols)
    d_query, dgain_q = norm_back(q_hat, q_inv, d_qnorm, gain_q)
    d_key, dgain_k = norm_back(k_hat, k_inv, d_knorm, gain_k)
    results = (
        jnp.stack([output, d_query, d_key, d_value], axis=2)
        .reshape(tile_rows, tile_cols, 4, feature_width)
        .astype(jnp.bfloat16)
    )
    received = shifted(results[tile_rows - window_size :], ROW, 1)
    results = lax.dynamic_slice_in_dim(
        jnp.concatenate([received, results], axis=0), window_size - shift_row, tile_rows, 0
    )
    received = shifted(results, COL, 1)
    results = lax.dynamic_slice_in_dim(
        jnp.concatenate([received, results], axis=1), window_size - shift_col, tile_cols, 1
    )
    attention = results[:, :, 0]
    d_qkv = results[:, :, 1:]
    table_local = jnp.einsum("hqk,qkc->hc", d_bias, one_hot, precision=lax.Precision.HIGHEST)
    totals = (over_axes(jnp.stack([dgain_q, dgain_k]), ROW_COL), over_axes(table_local, ROW_COL))
    return (attention, d_qkv, totals[0], totals[1].reshape(head_count, span_count, span_count))


def solution(mesh):
    torus = Mesh(mesh.devices.reshape(8, 2, 2, 4, 2), ("row_0", "row_1", "row_2", "col_0", "col_1"))
    placed = (P(ROW, COL, None, None), P(ROW, COL, None), P(), P(), P(), P())
    return jax.shard_map(
        local,
        mesh=torus,
        in_specs=placed,
        out_specs=(P(ROW, COL, None), P(ROW, COL, None, None), P(), P()),
        check_vma=False,
    )
```

profile of v0, /device:TPU:96, one launch (start us, length us, event | category | flops | bytes accessed | tf_op | source)
XLA Modules:
  0.0 300.2 jit_solution(13622738394343589350)
XLA Ops:
  0.6 1.5 pad_maximum_fusion
  2.2 2.1 collective-permute-start
  6.8 15.4 %collective-permute-done = bf16[8,8,4,3072]{3,1,2,0:T(8,128)(2,1)} collective-permute-done((bf16[8,8,4,3072]{3,1,2,0:T(8,128)(2,1)S(1)}, bf16[8,8,4,3072]{3,1,2,0:T(8,128)(2,1)}, u32[]{:S(2)}, u32[]{:S(2)}) %collective-permute-start) | collective-permute-done | bytes 1572896 | tf_op jit(solution)/shard_map/ppermute | solution.py:22
  22.2 2.9 fusion.5
  25.1 3.3 %collective-permute-start.1 = (bf16[16,8,4,3072]{3,1,2,0:T(8,128)(2,1)S(1)}, bf16[16,8,4,3072]{3,1,2,0:T(8,128)(2,1)}, u32[]{:S(2)}, u32[]{:S(2)}) collective-permute-start(bf16[16,8,4,3072]{3,1,2,0:T(8,128)(2,1)S(1)} %fusion.5), channel_id=1, source_target_pairs={{0,7},{1,0},{2,1},{3,2},{4,3},{5,4},{6,5},{7,6},{8,15},{9,8},{10,9... | collective-permute-start | bytes 9437192 | tf_op jit(solution)/shard_map/ppermute | solution.py:22
  31.9 0.9 iota_compare_fusion
  32.8 4.5 %fusion.20 = f32[24,64,64]{2,0,1:T(8,128)} fusion(pred[64,64,225]{2,0,1:T(32,128)(4,1)S(1)} %iota_compare_fusion, f32[24,225]{0,1:T(8,128)S(1)} %reshape.290), kind=kOutput, calls=%fused_computation.52 | convolution fusion | flops 265420800 | bytes 1336416 | tf_op jit(solution)/shard_map/hc,qkc->hqk/dot_general | solution.py:128
  37.3 2.3 copy.53
  41.5 54.5 %collective-permute-done.1 = bf16[16,8,4,3072]{3,1,2,0:T(8,128)(2,1)} collective-permute-done((bf16[16,8,4,3072]{3,1,2,0:T(8,128)(2,1)S(1)}, bf16[16,8,4,3072]{3,1,2,0:T(8,128)(2,1)}, u32[]{:S(2)}, u32[]{:S(2)}) %collective-permute-start.1) | collective-permute-done | bytes 3145760 | tf_op jit(solution)/shard_map/ppermute | solution.py:22
  96.0 4.0 %fusion.7 = bf16[16,8,4,3072]{3,1,2,0:T(8,128)(2,1)S(1)} fusion(s32[]{:T(128)S(6)} %select_n.71, bf16[16,8,4,3072]{3,1,2,0:T(8,128)(2,1)S(1)} %fusion.5, bf16[16,8,4,3072]{3,1,2,0:T(8,128)(2,1)} %collective-permute-done.1), kind=kLoop, calls=%fused_computation.17 | loop fusion | flops 6291456 | bytes 9437188 | tf_op jit(solution)/shard_map/concatenate | solution.py:143
  100.0 0.9 copy.76
  100.9 0.9 convert_reduce_fusion
  101.8 2.4 fusion.38
  104.3 1.9 fusion.12
  106.4 4.2 %add_select_fusion = f32[2,24,64,64]{2,3,1,0:T(8,128)S(1)} fusion(f32[24,64,64]{1,2,0:T(8,128)} %copy.53, pred[2,64,64]{1,2,0:T(8,128)(4,1)} %broadcast_compare_fusion, f32[2,64,24,128]{3,2,1,0:T(8,128)} %bitcast.113, f32[128]{0:T(128)S(1)} %get-tuple-element.43, f32[2,64,24]{1,2,0:T(8,128)S(1)} %copy.47, f32[2,64,24]{1,2,0:T(8,128)S(1)} %copy.45, ...), kind=kOutput, calls=%fused_computation.44 | convolution fusion | flops 54067200 | bytes 4383744 | tf_op jit(solution)/shard_map/wqhd,wkhd->whqk/dot_general | solution.py:84
  110.7 1.6 fusion.40
  112.3 3.6 %fusion.19 = bf16[2,64,24,128]{3,1,2,0:T(8,128)(2,1)} fusion(bf16[2,64,24,128]{3,2,1,0:T(8,128)(2,1)} %bitcast.120, f32[2,24,64]{2,1,0:T(8,128)S(1)} %get-tuple-element.46, f32[2,24,64,64]{2,3,1,0:T(8,128)} %copy-done.2), kind=kOutput, calls=%fused_computation.51 | convolution fusion | flops 51317824 | bytes 2371584 | tf_op jit(solution)/shard_map/whqk,wqhd->wkhd/dot_general | solution.py:106
  115.9 3.6 %fusion.18 = bf16[2,64,24,128]{3,1,2,0:T(8,128)(2,1)} fusion(bf16[2,64,24,128]{3,2,1,0:T(8,128)(2,1)} %bitcast.122, f32[2,24,64]{2,1,0:T(8,128)S(1)} %get-tuple-element.46, f32[2,24,64,64]{2,3,1,0:T(8,128)} %copy-done.2), kind=kOutput, calls=%fused_computation.50 | convolution fusion | flops 51317824 | bytes 2371584 | tf_op jit(solution)/shard_map/whqk,wkhd->wqhd/dot_general | solution.py:93
  119.5 2.5 copy.56
  122.1 2.2 stack.22
  124.2 2.5 copy.69
  126.8 2.2 stack.25
  128.9 2.6 multiply_reduce_fusion.2
  131.5 1.4 fusion.29
  133.7 4.8 %multiply_reduce_fusion = (f32[128]{0:T(128)}, f32[2,64,24]{1,2,0:T(8,128)S(1)}, f32[2,64,24]{1,2,0:T(8,128)S(1)}, f32[2,24,128,64]{2,3,1,0:T(8,128)}) fusion(f32[2,64,24,128]{3,2,1,0:T(8,128)S(1)} %bitcast.111, f32[2,64,24]{1,2,0:T(8,128)S(1)} %copy.50, f32[2,64,24]{1,2,0:T(8,128)S(1)} %copy.48, f32[128]{0:T(128)S(1)} %copy-done.20, ...), kind=kOutput, calls=%fused_computation.36 | convolution fusion | flops 55437184 | bytes 5187072 | tf_op jit(solution)/shard_map/whqk,wqhd->wkhd/dot_general | solution.py:103
  138.4 5.3 %multiply_reduce_fusion.1 = (f32[128]{0:T(128)}, f32[2,64,24]{1,2,0:T(8,128)S(1)}, f32[2,64,24]{1,2,0:T(8,128)S(1)}, f32[2,24,128,64]{2,3,1,0:T(8,128)}) fusion(f32[2,64,24,128]{3,2,1,0:T(8,128)S(1)} %bitcast.115, f32[2,64,24]{1,2,0:T(8,128)S(1)} %copy.47, f32[2,64,24]{1,2,0:T(8,128)S(1)} %copy.45, f32[128]{0:T(128)S(1)} %copy-done.19, ...), kind=kOutput, calls=%fused_computation.37 | convolution fusion | flops 55437184 | bytes 5187072 | tf_op jit(solution)/shard_map/whqk,wkhd->wqhd/dot_general | solution.py:99
  145.7 0.8 copy.63
  146.5 1.4 copy.66
  147.9 1.4 copy.67
  149.4 1.6 multiply_bitcast_fusion
  150.9 0.9 copy.64
  152.6 0.9 copy.60
  153.6 5.1 %multiply_convert_fusion = (bf16[16,8,1,24,128]{4,3,1,2,0:T(8,128)(2,1)}, bf16[16,8,1,24,128]{4,3,1,2,0:T(8,128)(2,1)}) fusion(f32[16,8,1,24,128]{4,3,1,2,0:T(8,128)S(1)} %bitcast.108, f32[16,8,24]{2,1,0:T(8,128)S(1)} %bitcast.129, f32[16,8,24]{2,1,0:T(8,128)S(1)} %get-tuple-element.54, f32[16,8,24]{2,1,0:T(8,128)S(1)} %bitcast.128, ...), kind=kLoop, calls=%fused_computation.38 | loop fusion | flops 7077888 | bytes 6390784 | tf_op jit(solution)/shard_map/convert.8
  158.7 1.5 stack.24
  160.8 1.0 copy-done.5
  161.9 1.5 copy-done
  163.5 1.0 collective-permute-start.2
  165.8 20.0 %collective-permute-done.2 = bf16[8,8,4,3072]{3,1,0,2:T(8,128)(2,1)} collective-permute-done((bf16[8,8,4,3072]{3,1,0,2:T(8,128)(2,1)S(1)}, bf16[8,8,4,3072]{3,1,0,2:T(8,128)(2,1)}, u32[]{:S(2)}, u32[]{:S(2)}) %collective-permute-start.2) | collective-permute-done | bytes 1572896 | tf_op jit(solution)/shard_map/ppermute | solution.py:22
  185.8 2.6 fusion.3
  190.4 2.8 convolution_bitcast_fusion
  193.2 29.4 %all-reduce = (f32[2,128]{1,0:T(2,128)S(1)}, f32[24,225]{1,0:T(8,128)S(1)}) all-reduce(f32[2,128]{1,0:T(2,128)S(1)} %pad_maximum_fusion.1, f32[24,225]{1,0:T(8,128)S(1)} %convolution_bitcast_fusion), channel_id=1, replica_groups=mesh['row_0'=8,'row_1'=2,'row_2'=2,'col_0'=4,'col_1'=2] {'row_0'}, use_global_device_ids=true, to_apply=%region_13.14 | all-reduce | flops 5656 | bytes 45248 | tf_op jit(solution)/shard_map/psum | solution.py:26
  222.5 37.9 %all-reduce.4 = (f32[2,128]{1,0:T(2,128)S(1)}, f32[24,225]{1,0:T(8,128)S(1)}) all-reduce(f32[2,128]{1,0:T(2,128)S(1)} %get-tuple-element.22, f32[24,225]{1,0:T(8,128)S(1)} %get-tuple-element.23), channel_id=1, replica_groups=mesh['row_0'=8,'row_1'=2,'row_2'=2,'col_0'=4,'col_1'=2] {'row_1'}, use_global_device_ids=true, to_apply=%region_14.15 | all-reduce | flops 5656 | bytes 45248 | tf_op jit(solution)/shard_map/psum | solution.py:26
  260.4 3.7 %all-reduce.3 = (f32[2,128]{1,0:T(2,128)S(1)}, f32[24,225]{1,0:T(8,128)S(1)}) all-reduce(f32[2,128]{1,0:T(2,128)S(1)} %get-tuple-element.30, f32[24,225]{1,0:T(8,128)S(1)} %get-tuple-element.31), channel_id=1, replica_groups=mesh['row_0'=8,'row_1'=2,'row_2'=2,'col_0'=4,'col_1'=2] {'row_2'}, use_global_device_ids=true, to_apply=%region_15.16 | all-reduce | flops 5656 | bytes 45248 | tf_op jit(solution)/shard_map/psum | solution.py:26
  264.1 18.5 %all-reduce.1 = (f32[2,128]{1,0:T(2,128)S(1)}, f32[24,225]{1,0:T(8,128)S(1)}) all-reduce(f32[2,128]{1,0:T(2,128)S(1)} %get-tuple-element.28, f32[24,225]{1,0:T(8,128)S(1)} %get-tuple-element.29), channel_id=1, replica_groups=mesh['row_0'=8,'row_1'=2,'row_2'=2,'col_0'=4,'col_1'=2] {'col_0'}, use_global_device_ids=true, to_apply=%region_16.17 | all-reduce | flops 5656 | bytes 45248 | tf_op jit(solution)/shard_map/psum | solution.py:26
  282.8 10.0 %all-reduce.2 = (f32[2,128]{1,0:T(2,128)}, f32[24,15,15]{2,1,0:T(8,128)S(1)}) all-reduce(f32[2,128]{1,0:T(2,128)S(1)} %get-tuple-element.24, f32[24,15,15]{2,1,0:T(8,128)S(1)} %reshape.285), channel_id=1, replica_groups=mesh['row_0'=8,'row_1'=2,'row_2'=2,'col_0'=4,'col_1'=2] {'col_1'}, use_global_device_ids=true, to_apply=%region_17.18 | all-reduce | flops 5656 | bytes 45248 | tf_op jit(solution)/shard_map/psum | solution.py:26
  293.5 4.0 %fusion.6 = bf16[16,8,4,3072]{3,1,0,2:T(8,128)(2,1)S(1)} fusion(s32[]{:T(128)S(6)} %select_n.80, bf16[16,8,4,3072]{3,1,0,2:T(8,128)(2,1)} %collective-permute-done.3, bf16[16,8,4,3072]{3,1,0,2:T(8,128)(2,1)S(1)} %fusion.3), kind=kLoop, calls=%fused_computation.16 | loop fusion | flops 6291456 | bytes 9437188 | tf_op jit(solution)/shard_map/concatenate | solution.py:177
  297.6 0.9 slice_bitcast_fusion
  298.7 1.6 copy.71
  (76 shorter events, 9.1 us)
Async XLA Ops:
  0.6 3.6 %copy-start.16 = (s32[2]{0:T(128)S(1)}, s32[2]{0:T(128)}, u32[]{:S(2)}) copy-start(s32[2]{0:T(128)} %param.10) | copy-start | bytes 28
  2.2 20.0 %collective-permute-start = (bf16[8,8,4,3072]{3,1,2,0:T(8,128)(2,1)S(1)}, bf16[8,8,4,3072]{3,1,2,0:T(8,128)(2,1)}, u32[]{:S(2)}, u32[]{:S(2)}) collective-permute-start(bf16[8,8,4,3072]{3,1,2,0:T(8,128)(2,1)S(1)} %pad_maximum_fusion), channel_id=1, source_target_pairs={{0,248},{8,0},{16,8},{24,16},{32,24},{40,32},{48,40},{56,48},{64,5... | collective-permute-start | bytes 4718600 | tf_op jit(solution)/shard_map/ppermute | solution.py:22
  6.8 24.0 %copy-start.14 = (f32[24,15,15]{0,2,1:T(8,128)S(1)}, f32[24,15,15]{0,2,1:T(8,128)}, u32[]{:S(2)}) copy-start(f32[24,15,15]{0,2,1:T(8,128)} %param.9) | copy-start | bytes 64804
  6.8 24.1 %copy-start.13 = (s32[512,64]{0,1:T(8,128)S(1)}, s32[512,64]{0,1:T(8,128)}, u32[]{:S(2)}) copy-start(s32[512,64]{0,1:T(8,128)} %param.11) | copy-start | bytes 393220
  25.1 70.9 %collective-permute-start.1 = (bf16[16,8,4,3072]{3,1,2,0:T(8,128)(2,1)S(1)}, bf16[16,8,4,3072]{3,1,2,0:T(8,128)(2,1)}, u32[]{:S(2)}, u32[]{:S(2)}) collective-permute-start(bf16[16,8,4,3072]{3,1,2,0:T(8,128)(2,1)S(1)} %fusion.5), channel_id=1, source_target_pairs={{0,7},{1,0},{2,1},{3,2},{4,3},{5,4},{6,5},{7,6},{8,15},{9,8},{10,9... | collective-permute-start | bytes 9437192 | tf_op jit(solution)/shard_map/ppermute | solution.py:22
  31.3 0.6 copy-start.11
  37.3 2.9 copy-start.15
  110.6 1.7 copy-start.2
  128.9 2.6 copy-start.1
  131.5 1.4 copy-start.3
  131.5 2.2 copy-start.4
  131.5 2.1 copy-start.20
  133.7 4.8 %copy-start.19 = (f32[128]{0:T(128)S(1)}, f32[128]{0:T(128)}, u32[]{:S(2)}) copy-start(f32[128]{0:T(128)} %get-tuple-element.41) | copy-start | bytes 1540
  150.9 1.4 copy-start.8
  152.6 0.9 copy-start.9
  152.6 0.9 copy-start.10
  158.7 1.6 copy-start.7
  158.7 1.9 copy-start.6
  160.6 1.1 copy-start.5
  161.8 1.7 copy-start
  163.5 22.4 %collective-permute-start.2 = (bf16[8,8,4,3072]{3,1,0,2:T(8,128)(2,1)S(1)}, bf16[8,8,4,3072]{3,1,0,2:T(8,128)(2,1)}, u32[]{:S(2)}, u32[]{:S(2)}) collective-permute-start(bf16[8,8,4,3072]{3,1,0,2:T(8,128)(2,1)S(1)} %slice.56), channel_id=1, source_target_pairs={{0,8},{8,16},{16,24},{24,32},{32,40},{40,48},{48,56},{56,64},{64,7... | collective-permute-start | bytes 4718600 | tf_op jit(solution)/shard_map/ppermute | solution.py:22
  165.8 24.5 %copy-start.17 = (f32[128]{0:T(128)S(1)}, f32[128]{0:T(128)}, u32[]{:S(2)}) copy-start(f32[128]{0:T(128)} %get-tuple-element.14) | copy-start | bytes 1540
  165.8 24.5 %copy-start.18 = (f32[128]{0:T(128)S(1)}, f32[128]{0:T(128)}, u32[]{:S(2)}) copy-start(f32[128]{0:T(128)} %get-tuple-element.12) | copy-start | bytes 1540
  165.8 24.5 %copy-start.12 = (s32[64,64]{0,1:T(8,128)S(1)}, s32[64,64]{0,1:T(8,128)}, u32[]{:S(2)}) copy-start(s32[64,64]{0,1:T(8,128)} %copy-done.11) | copy-start | bytes 49156
  188.4 105.1 %collective-permute-start.3 = (bf16[16,8,4,3072]{3,1,0,2:T(8,128)(2,1)S(1)}, bf16[16,8,4,3072]{3,1,0,2:T(8,128)(2,1)}, u32[]{:S(2)}, u32[]{:S(2)}) collective-permute-start(bf16[16,8,4,3072]{3,1,0,2:T(8,128)(2,1)S(1)} %fusion.3), channel_id=1, source_target_pairs={{0,1},{1,2},{2,3},{3,4},{4,5},{5,6},{6,7},{7,0},{8,9},{9,10},{10,1... | collective-permute-start | bytes 9437192 | tf_op jit(solution)/shard_map/ppermute | solution.py:22
where the time goes:
time: 302 us; the launch traced here: 300 us
  blocking collectives  99.4 us (33%)
  waiting for transfers between devices  89.9 us (30%)
  other arithmetic  34.4 us (11%)
  matrix products  31.4 us (10%)
  local copies, waits for them, and re-layouts  29.4 us (10%)
  between operations  8.49 us (3%)
  starting transfers between devices  7.13 us (2%)
    psum x5, blocking collectives, over_axes(): return functools.reduce(lax.psum, axes, array)  99.4 us
    ppermute x4, waiting for transfers between devices, shifted(): return lax.ppermute(value, axis, pairs)  89.9 us
    unnamed x48, local copies, waits for them, and re-layouts  7.83 us
    ppermute x4, starting transfers between devices, shifted(): return lax.ppermute(value, axis, pairs)  7.13 us
    another operation x5, local copies, waits for them, and re-layouts, local(): jnp.stack([output, d_query, d_key, d_value], axis=2)  6.26 us
  transfers between devices with their start and end apart: 4, of which 3 were waited for; matrix products, arithmetic and copies ran while one was open for 5% of the time, Pallas kernels for 0%

commit v1 on v0

v1 whole, which is shorter than its diff:
```python
import functools
import math

import jax
import jax.numpy as jnp
from jax import lax
from jax.experimental import pallas as pl
from jax.experimental.pallas import tpu as pltpu
from jax.sharding import Mesh
from jax.sharding import PartitionSpec as P

ROW = ("row_0", "row_1", "row_2")
COL = ("col_0", "col_1")
ROW_COL = ("row_0", "row_1", "row_2", "col_0", "col_1")

EPSILON = 1e-06
NEG_FILL = -1e30
WIN = 8
HALF = 4
HD = 128
STEP_HEADS = 4


def shifted(value, axis, steps):
    count = lax.axis_size(axis)
    pairs = [(source, (source + steps) % count) for source in range(count)]
    return lax.ppermute(value, axis, pairs)


def pulled(slot, shift, extent):
    low = jnp.where(shift <= HALF, 0, shift + extent - WIN)
    return (slot >= low) & (slot < jnp.where(shift <= HALF, shift, extent))


def head_norm(values, gain_vec):
    centred = values - jnp.mean(values, axis=-1, keepdims=True)
    variance = jnp.mean(centred * centred, axis=-1, keepdims=True)
    inv_sigma = lax.rsqrt(variance + EPSILON)
    x_hat = centred * inv_sigma
    return x_hat, inv_sigma, (x_hat * gain_vec).astype(jnp.bfloat16)


def norm_back(x_hat, inv_sigma, d_hat):
    first_mean = jnp.mean(d_hat, axis=-1, keepdims=True)
    second_mean = jnp.mean(d_hat * x_hat, axis=-1, keepdims=True)
    return inv_sigma * (d_hat - first_mean - x_hat * second_mean)


def fold_rows(values):
    return functools.reduce(jnp.add, [values[i * 8 : i * 8 + 8] for i in range(values.shape[0] // 8)])


def matmul(left, right, left_dim, right_dim, **kwargs):
    return lax.dot_general(
        left, right, (((left_dim,), (right_dim,)), ((), ())), preferred_element_type=jnp.float32, **kwargs
    )


def window_kernel(
    spec, qkv, cot, hcol, hrow, table, gains, labels, att, dqkv, sums, x_all, mask, table_grad, gain_grad
):
    step = pl.program_id(0)
    steps = pl.num_programs(0)
    shift_row, shift_col, grid_row, grid_col = spec[0], spec[1], spec[2], spec[3]
    tokens = 128
    col_place = lambda col: (col - shift_col) & 7
    score_scale = 1.0 / math.sqrt(HD)

    @pl.when(step == 0)
    def _():
        cols = labels.shape[0]
        rows = labels.shape[1]
        col_turn = jnp.where(shift_col <= HALF, WIN, cols - WIN)
        row_turn = jnp.where(shift_row <= HALF, 16, rows - 16)
        lane = lax.broadcasted_iota(jnp.int32, (8, 128), 1)
        sub = lax.broadcasted_iota(jnp.int32, (8, 128), 0)

        def labels_at(first_row):
            base = pl.multiple_of((first_row // 128) * 128, 128)
            here = labels[pl.ds(pl.multiple_of(grid_col, 8), 8), pl.ds(base, 128)]
            there = labels[pl.ds(pl.multiple_of((grid_col + col_turn) % cols, 8), 8), pl.ds(base, 128)]
            both = jnp.where(pulled(sub, shift_col, WIN), there, here).astype(jnp.float32)
            return pltpu.roll(both, (128 - first_row % 128) % 128, 1)

        slots = jnp.where(
            pulled(lane, shift_row, 16), labels_at((grid_row + row_turn) % rows), labels_at(grid_row)
        )
        across = jnp.concatenate([jnp.broadcast_to(slots[:, i : i + 1], (8, 128)) for i in range(16)], axis=0)
        query = lax.broadcasted_iota(jnp.int32, (tokens, tokens), 0) // 8
        key = lax.broadcasted_iota(jnp.int32, (tokens, tokens), 1) // 8
        same = (((query - shift_row) & 15) // 8) == (((key - shift_row) & 15) // 8)
        mask[...] = jnp.where(same & (across == across.T), 0.0, NEG_FILL)
        gain_grad[...] = jnp.zeros_like(gain_grad)

    def comp(ref, row, part, lanes):
        return ref[row, part, :, lanes] if ref is not cot else ref[row, :, lanes]

    for head in range(STEP_HEADS):
        lanes = slice(head * HD, head * HD + HD)
        for part in range(4):
            source = qkv if part < 3 else cot
            for row in range(16):
                x_all[head * 4 + part, row * 8 : row * 8 + 8, :] = comp(source, row, part, lanes).astype(jnp.float32)
    for i in range(HALF):
        row = jnp.where(shift_row <= HALF, i, i + 12)

        @pl.when(pulled(row, shift_row, 16))
        def _():
            start = pl.multiple_of(row * 8, 8)
            for head in range(STEP_HEADS):
                lanes = slice(head * HD, head * HD + HD)
                for part in range(4):
                    x_all[head * 4 + part, pl.ds(start, 8), :] = hrow[i, part, :, lanes].astype(jnp.float32)

    for i in range(HALF):
        col = jnp.where(shift_col <= HALF, i, i + HALF)

        @pl.when(pulled(col, shift_col, WIN))
        def _():
            for head in range(STEP_HEADS):
                lanes = slice(head * HD, head * HD + HD)
                for part in range(4):
                    x_all[head * 4 + part, pl.ds(col, 16, stride=8), :] = hcol[i, part, :, lanes].astype(jnp.float32)

    sub = lax.broadcasted_iota(jnp.int32, (8, 128), 0)
    lane = lax.broadcasted_iota(jnp.int32, (8, 128), 1)
    col_code = col_place(sub) - col_place(lane & 7) + WIN - 1
    gain_q = gains[0:1, :]
    gain_k = gains[1:2, :]
    for head in range(STEP_HEADS):
        lanes = slice(head * HD, head * HD + HD)
        q_hat, q_inv, q_norm = head_norm(x_all[head * 4], gain_q)
        k_hat, k_inv, k_norm = head_norm(x_all[head * 4 + 1], gain_k)
        values = x_all[head * 4 + 2].astype(jnp.bfloat16)
        grads = x_all[head * 4 + 3].astype(jnp.bfloat16)
        diagonal = jnp.zeros((8, 128), jnp.float32)
        for y in range(15):
            diagonal = jnp.where(col_code == y, table[head, y : y + 1, :], diagonal)
        bias = jnp.concatenate([pltpu.roll(diagonal, (row * 8 - 56) % 128, 1) for row in range(16)], axis=0)
        scores = matmul(q_norm, k_norm, 1, 1) * score_scale + bias + mask[...]
        weights = jnp.exp(scores - jnp.max(scores, axis=-1, keepdims=True))
        probs = weights * (1.0 / jnp.sum(weights, axis=-1, keepdims=True))
        probs_b = probs.astype(jnp.bfloat16)
        att[:, :, lanes] = matmul(probs_b, values, 1, 0).reshape(16, 8, HD).astype(jnp.bfloat16)
        d_probs = matmul(grads, values, 1, 1)
        row_dot = jnp.sum(probs * d_probs, axis=-1, keepdims=True)
        d_scores = probs * (d_probs - row_dot)
        d_scores_b = d_scores.astype(jnp.bfloat16)
        folded = functools.reduce(
            jnp.add,
            [pltpu.roll(d_scores[row * 8 : row * 8 + 8], (56 - row * 8) % 128, 1) for row in range(16)],
        )
        by_code = [jnp.sum(jnp.where(col_code == y, folded, 0.0), axis=0, keepdims=True) for y in range(15)]
        table_grad[pl.ds(pl.multiple_of((step * STEP_HEADS + head) * 16, 16), 16), :] = jnp.concatenate(
            by_code + [jnp.zeros((1, 128), jnp.float32)], axis=0
        )
        dqkv[:, 2, :, lanes] = matmul(probs_b, grads, 0, 0).reshape(16, 8, HD).astype(jnp.bfloat16)
        d_qnorm = matmul(d_scores_b, k_norm, 1, 0)
        gain_grad[0] += fold_rows(d_qnorm * q_hat)
        d_query = norm_back(q_hat, q_inv, d_qnorm * (gain_q * score_scale))
        dqkv[:, 0, :, lanes] = d_query.reshape(16, 8, HD).astype(jnp.bfloat16)
        d_knorm = matmul(d_scores_b, q_norm, 0, 0)
        gain_grad[1] += fold_rows(d_knorm * k_hat)
        d_key = norm_back(k_hat, k_inv, d_knorm * (gain_k * score_scale))
        dqkv[:, 1, :, lanes] = d_key.reshape(16, 8, HD).astype(jnp.bfloat16)

    @pl.when(step == steps - 1)
    def _():
        group = lax.broadcasted_iota(jnp.int32, (16, 128), 0)
        member = lax.broadcasted_iota(jnp.int32, (16, 128), 1) // 8
        pick = jnp.where((group == member) & (group < 15), 1.0, 0.0)
        by_offset = matmul(pick, table_grad[...], 1, 1, precision=lax.Precision.HIGHEST)
        gain_q_sum = jnp.sum(gain_grad[0], axis=0, keepdims=True) * score_scale
        gain_k_sum = jnp.sum(gain_grad[1], axis=0, keepdims=True) * score_scale
        last = jnp.concatenate([gain_q_sum, gain_k_sum, jnp.zeros_like(gain_k_sum)], axis=1)
        is_last = lax.broadcasted_iota(jnp.int32, by_offset.shape, 0) == 15
        sums[...] = jnp.where(is_last, last, by_offset)


def run_windows(spec, qkv, cot, hcol, hrow, table, gains, labels):
    head_count = table.shape[0]
    width = STEP_HEADS * HD
    return pl.pallas_call(
        window_kernel,
        grid_spec=pltpu.PrefetchScalarGridSpec(
            num_scalar_prefetch=1,
            grid=(head_count // STEP_HEADS,),
            in_specs=[
                pl.BlockSpec((16, 3, 8, width), lambda i, s: (0, 0, 0, i)),
                pl.BlockSpec((16, 8, width), lambda i, s: (0, 0, i)),
                pl.BlockSpec((HALF, 4, 16, width), lambda i, s: (0, 0, 0, i)),
                pl.BlockSpec((HALF, 4, 8, width), lambda i, s: (0, 0, 0, i)),
                pl.BlockSpec((STEP_HEADS, 16, 128), lambda i, s: (i, 0, 0)),
                pl.BlockSpec((2, 128), lambda i, s: (0, 0)),
                pl.BlockSpec(labels.shape, lambda i, s: (0, 0)),
            ],
            out_specs=[
                pl.BlockSpec((16, 8, width), lambda i, s: (0, 0, i)),
                pl.BlockSpec((16, 3, 8, width), lambda i, s: (0, 0, 0, i)),
                pl.BlockSpec((16, head_count * 16), lambda i, s: (0, 0)),
            ],
            scratch_shapes=[
                pltpu.VMEM((STEP_HEADS * 4, 128, HD), jnp.float32),
                pltpu.VMEM((128, 128), jnp.float32),
                pltpu.VMEM((head_count * 16, 128), jnp.float32),
                pltpu.VMEM((2, 8, 128), jnp.float32),
            ],
        ),
        out_shape=[
            jax.ShapeDtypeStruct(cot.shape, jnp.bfloat16),
            jax.ShapeDtypeStruct(qkv.shape, jnp.bfloat16),
            jax.ShapeDtypeStruct((16, head_count * 16), jnp.float32),
        ],
        compiler_params=pltpu.CompilerParams(dimension_semantics=("arbitrary",)),
        name="windows",
    )(spec, qkv, cot, hcol, hrow, table, gains, labels)


def exchange(shift, extent, axis, towards_owner, pieces):
    def branch(s):
        low, high, steps = (0, s, -1) if s <= HALF else (s + extent - WIN, extent, 1)
        if towards_owner:
            steps = -steps

        def run():
            received = shifted(pieces(low, high), axis, steps)
            first = low % HALF
            spare = (first, HALF - first - (high - low), 0)
            return lax.pad(received, jnp.zeros((), received.dtype), (spare,) + ((0, 0, 0),) * (received.ndim - 1))

        return run

    return lax.switch(shift - 1, [branch(s) for s in range(1, WIN)])


def stack_parts(qkv, cot):
    return jnp.concatenate([qkv, cot[:, None]], axis=1)


def fill_rows(own, strip, shift_row):
    slot = lax.broadcasted_iota(jnp.int32, own.shape, 0)
    zeros = jnp.zeros((16 - 2 * HALF,) + own.shape[1:], own.dtype)
    return jnp.where(pulled(slot, shift_row, 16), jnp.concatenate([strip, zeros, strip], axis=0), own)


def fill_cols(own, strip, shift_col):
    slot = lax.broadcasted_iota(jnp.int32, own.shape, 2)
    turned = jnp.transpose(strip, (2, 1, 0, 3))
    return jnp.where(pulled(slot, shift_col, WIN), jnp.concatenate([turned, turned], axis=2), own)


def local(qkv, cotangent, norm_gains, rel_table, shifts, mask_ids):
    head_count = rel_table.shape[0]
    shift_row = shifts[0]
    shift_col = shifts[1]
    spec = jnp.stack([shift_row, shift_col, lax.axis_index(ROW) * 16, lax.axis_index(COL) * 8]).astype(jnp.int32)
    qkv_t = jnp.transpose(qkv, (0, 2, 1, 3))
    by_col = jnp.transpose(jnp.flip(rel_table, 1), (0, 2, 1))
    table = jnp.pad(jnp.repeat(by_col, 8, axis=2), ((0, 0), (0, 1), (0, 8)))

    hrow = exchange(shift_row, 16, ROW, False, lambda a, b: stack_parts(qkv_t[a:b], cotangent[a:b]))
    filled = fill_rows(stack_parts(qkv_t, cotangent), hrow, shift_row)
    hcol = exchange(shift_col, WIN, COL, False, lambda a, b: jnp.transpose(filled[:, :, a:b], (2, 1, 0, 3)))
    att, dqkv, sums = run_windows(spec, qkv_t, cotangent, hcol, hrow, table, norm_gains, mask_ids.T)
    back_row = exchange(shift_row, 16, ROW, True, lambda a, b: stack_parts(dqkv[a:b], att[a:b]))
    filled = fill_rows(stack_parts(dqkv, att), back_row, shift_row)
    back_col = exchange(shift_col, WIN, COL, True, lambda a, b: jnp.transpose(filled[:, :, a:b], (2, 1, 0, 3)))
    merged = fill_cols(filled, back_col, shift_col)
    sums = lax.psum(sums, ROW_COL)
    d_gains = sums[15, : 2 * HD].reshape(2, HD)
    d_table = jnp.transpose(jnp.flip(sums[:15], 0).reshape(15, head_count, 16)[:, :, :15], (1, 0, 2))
    return (merged[:, 3], jnp.transpose(merged[:, :3], (0, 2, 1, 3)), d_gains, d_table)


def solution(mesh):
    torus = Mesh(mesh.devices.reshape(8, 2, 2, 4, 2), ROW_COL)
    placed = (P(ROW, COL, None, None), P(ROW, COL, None), P(), P(), P(), P())
    return jax.shard_map(
        local,
        mesh=torus,
        in_specs=placed,
        out_specs=(P(ROW, COL, None), P(ROW, COL, None, None), P(), P()),
        check_vma=False,
    )
```

time: 302 us -> 221 us (0.73)
  waiting for transfers between devices: 89.9 us -> 53.8 us
  matrix products: 31.4 us -> 0 us
  other arithmetic: 34.4 us -> 11 us
  Pallas kernels: 0 us -> 22.1 us
  loops' own time: 0 us -> 21.2 us
  blocking collectives: 99.4 us -> 80.5 us
  local copies, waits for them, and re-layouts: 29.4 us -> 23.5 us
  starting transfers between devices: 7.13 us -> 2.74 us
    ppermute x4, waiting for transfers between devices: 89.9 us -> 53.8 us  [shifted(): return lax.ppermute(value, axis, pairs)]
    dot_general x8 -> x0, matrix products: 31.4 us -> none  [the longest x1 5.32 us: window_core(): jnp.einsum('whqk,wkhd->wqhd', d_scores_b, k_norm, preferred_element_type=...]
    pallas_call x0 -> x1, Pallas kernels: none -> 22.1 us  [run_windows(): pl.pallas_call(window_kernel, grid_spec=pltpu.PrefetchScalarGridSpec(num_...]
    another operation x0 -> x4, loops' own time: none -> 21.2 us  [exchange(): return lax.switch(shift - 1, [branch(s) for s in range(1, WIN)])]
    psum x5 -> x1, blocking collectives: 99.4 us -> 80.5 us  [local(): sums = lax.psum(sums, ROW_COL)]
    concatenate x7 -> x3, other arithmetic: 15.2 us -> 3.9 us  [the longest x1 3.79 us: fill_rows(): jnp.concatenate([strip, zeros, strip], axis=0)]
    unnamed x48 -> x13, local copies, waits for them, and re-layouts: 7.83 us -> 0.84 us
    select_n x1 -> x2, other arithmetic: 0.01 us -> 6.26 us  [the longest x1 3.85 us: fill_cols(): jnp.where(pulled(slot, shift_col, WIN), jnp.concatenate([turned, turned],...]
  transfers between devices with their start and end apart: 4 -> 4, of which waited for: 3 -> 4; matrix products, arithmetic and copies ran while one was open for 5% -> 0% of each run, Pallas kernels for 0% -> 0%
where the time goes in v1:
time: 221 us
  blocking collectives  80.5 us (36%)
  waiting for transfers between devices  53.8 us (24%)
  local copies, waits for them, and re-layouts  23.5 us (11%)
  Pallas kernels  22.1 us (10%)
  loops' own time  21.2 us (10%)
  other arithmetic  11 us (5%)
  between operations  6.23 us (3%)
  starting transfers between devices  2.74 us (1%)
    psum x1, blocking collectives, local(): sums = lax.psum(sums, ROW_COL)  80.5 us
    ppermute x4, waiting for transfers between devices, shifted(): return lax.ppermute(value, axis, pairs)  53.8 us
    pallas_call x1, Pallas kernels, run_windows(): pl.pallas_call(window_kernel, grid_spec=pltpu.PrefetchScalarGridSpec(num_...  22.1 us
    another operation x4, loops' own time, exchange(): return lax.switch(shift - 1, [branch(s) for s in range(1, WIN)])  21.2 us
    pad x4, local copies, waits for them, and re-layouts, run(): lax.pad(received, jnp.zeros((), received.dtype), (spare,) + ((0, 0, 0),)...  4.54 us
  transfers between devices with their start and end apart: 4, of which 4 were waited for; matrix products, arithmetic and copies ran while one was open for 0% of the time, Pallas kernels for 0%

profile of v1, /device:TPU:96, one launch (start us, length us, event | category | flops | bytes accessed | tf_op | source)
XLA Modules:
  0.0 221.1 jit_solution(3215551016716323534)
XLA Ops:
  0.6 1.3 fusion.7
  4.6 14.8 %conditional.4 = (bf16[4,4,8,3072]{3,2,1,0:T(8,128)(2,1)}) conditional(s32[]{:T(128)} %clamp.9, (bf16[16,3,8,3072]{3,2,1,0:T(8,128)(2,1)}, bf16[16,8,3072]{2,1,0:T(8,128)(2,1)}) %tuple.142, (bf16[16,3,8,3072]{3,2,1,0:T(8,128)(2,1)}, bf16[16,8,3072]{2,1,0:T(8,128)(2,1)}) %tuple.143, ...), branch_computations={%region_0.1_spmd, %region_1.2_spmd, %region_2.3_spmd, %region_3.4_... | conditional | flops 393216 | bytes 6291504 | solution.py:233
  4.6 1.0 slice.107
  5.6 0.9 slice_bitcast_fusion.4
  6.6 0.1 pad_maximum_fusion.4
  6.6 0.1 collective-permute-start.4
  6.7 11.7 %collective-permute-done.4 = bf16[3,4,8,3072]{3,2,1,0:T(8,128)(2,1)S(1)} collective-permute-done((bf16[3,4,8,3072]{3,2,1,0:T(8,128)(2,1)S(1)}, bf16[3,4,8,3072]{3,2,1,0:T(8,128)(2,1)S(1)}, u32[]{:S(2)}, u32[]{:S(2)}) %collective-permute-start.4) | collective-permute-done | bytes 589856 | tf_op jit(solution)/shard_map/cond/branch_4_fun/ppermute | solution.py:27
  18.4 1.0 pad.54
  19.4 0.1 pad.115.clone
  19.5 3.8 %pad_maximum_fusion.14 = (bf16[16,4,8,3072]{3,2,1,0:T(8,128)(2,1)S(1)}, bf16[16,4,8,3072]{3,2,1,0:T(8,128)(2,1)}) fusion(bf16[4,4,8,3072]{3,2,1,0:T(8,128)(2,1)} %get-tuple-element.243.hrow, bf16[16]{0:T(256)(128)(2,1)S(1)} %pad.115.clone, bf16[16,1,8,3072]{3,2,1,0:T(8,128)(2,1)} %bitcast.88, bf16[16,3,8,3072]{3,2,1,0:T(8,128)(2,1)} %bitcast.86), kind=kLoop, calls=%fused_computation.49 | loop fusion | flops 4718592 | bytes 10223648 | tf_op jit(solution)/shard_map/concatenate | solution.py:243
  23.9 0.0 copy-start.12
  23.9 0.0 copy-start.10
  23.9 45.8 %conditional.5 = (bf16[4,4,16,3072]{3,2,1,0:T(8,128)(2,1)}) conditional(s32[]{:T(128)} %clamp.8, (pred[16]{0:T(512)(128)(4,1)S(1)}, bf16[16,4,8,3072]{3,2,1,0:T(8,128)(2,1)S(1)}, bf16[16,4,8,3072]{3,2,1,0:T(8,128)(2,1)}) %tuple.100, (pred[16]{0:T(512)(128)(4,1)S(1)}, bf16[16,4,8,3072]{3,2,1,0:T(8,128)(2,1)S(1)}, ...), branch_computations={%region_7.8_spmd, %region_8.9_spmd, %region_9.10_spmd, %region_10.... | conditional | flops 786432 | bytes 36175968 | solution.py:233
  34.7 1.7 copy.27
  36.5 0.1 copy-done.5
  36.6 1.7 copy.28
  38.3 0.1 fusion.5
  38.5 1.6 collective-permute-start.12
  40.0 18.3 %collective-permute-done.12 = bf16[2,4,16,3072]{3,2,1,0:T(8,128)(2,1)S(1)} collective-permute-done((bf16[2,4,16,3072]{3,2,1,0:T(8,128)(2,1)S(1)}, bf16[2,4,16,3072]{3,2,1,0:T(8,128)(2,1)S(1)}, u32[]{:S(2)}, u32[]{:S(2)}) %collective-permute-start.12) | collective-permute-done | bytes 786464 | tf_op jit(solution)/shard_map/cond/branch_5_fun/ppermute | solution.py:27
  58.4 1.3 pad.61
  69.8 0.0 copy-start.9
  69.8 0.7 pad_add_fusion.spec
  70.5 0.1 broadcast_bitcast_fusion
  70.6 0.3 copy.32
  70.9 0.7 pad.76.table
  71.6 22.1 %windows.1 = (bf16[16,8,3072]{2,1,0:T(8,128)(2,1)S(1)}, bf16[16,3,8,3072]{3,2,1,0:T(8,128)(2,1)}, f32[16,384]{1,0:T(8,128)}) custom-call(s32[4]{0:T(128)} %pad_add_fusion.spec, bf16[16,3,8,3072]{3,2,1,0:T(8,128)(2,1)S(1)} %bitcast.87, bf16[16,8,3072]{2,1,0:T(8,128)(2,1)} %cot.1, bf16[4,4,16,3072]{3,2,1,0:T(8,128)(2,1)} %get-tuple-element.244.hcol, ...), custom_call_target="tpu_custom_call" | custom-call | tf_op jit(solution)/shard_map/windows/pallas_call | solution.py:183
  93.7 9.6 %conditional.6 = (bf16[4,4,8,3072]{3,2,1,0:T(8,128)(2,1)}) conditional(s32[]{:T(128)} %clamp.9, (bf16[16,3,8,3072]{3,2,1,0:T(8,128)(2,1)}, bf16[16,8,3072]{2,1,0:T(8,128)(2,1)S(1)}) %tuple.101, (bf16[16,3,8,3072]{3,2,1,0:T(8,128)(2,1)}, bf16[16,8,3072]{2,1,0:T(8,128)(2,1)S(1)}) %tuple.101, ...), branch_computations={%region_14.15_spmd, %region_15.16_spmd, %region_16.17_spmd, %regio... | conditional | flops 393216 | bytes 6291504 | solution.py:233
  93.7 1.0 slice.128
  94.7 0.1 pad_maximum_fusion.11
  94.8 0.1 collective-permute-start.18
  94.9 7.4 %collective-permute-done.18 = bf16[3,4,8,3072]{3,2,1,0:T(8,128)(2,1)S(1)} collective-permute-done((bf16[3,4,8,3072]{3,2,1,0:T(8,128)(2,1)S(1)}, bf16[3,4,8,3072]{3,2,1,0:T(8,128)(2,1)S(1)}, u32[]{:S(2)}, u32[]{:S(2)}) %collective-permute-start.18) | collective-permute-done | bytes 589856 | tf_op jit(solution)/shard_map/cond/branch_4_fun/ppermute | solution.py:27
  102.3 1.0 pad.66
  103.2 2.4 %maximum_select_fusion = bf16[16,4,8,3072]{3,2,1,0:T(8,128)(2,1)S(1)} fusion(bf16[4,4,8,3072]{3,2,1,0:T(8,128)(2,1)} %get-tuple-element.245, bf16[16,1,8,3072]{3,2,1,0:T(8,128)(2,1)S(1)} %bitcast.90, bf16[16,3,8,3072]{3,2,1,0:T(8,128)(2,1)} %get-tuple-element.207, pred[16]{0:T(512)(128)(4,1)S(1)} %compare_and_fusion, bf16[16]{0:T(256)(128)(2,1)S(1)} %pad.115.clone), kind=kLoop, calls=%fused_computation.51 | loop fusion | flops 6291456 | bytes 7077936 | tf_op jit(solution)/shard_map/jit(_where)/select_n | solution.py:243
  105.7 1.7 copy.33
  107.4 19.0 %conditional.7 = (bf16[4,4,16,3072]{3,2,1,0:T(8,128)(2,1)}) conditional(s32[]{:T(128)} %clamp.8, bf16[16,4,8,3072]{3,0,1,2:T(8,128)(2,1)S(1)} %copy.33, bf16[16,4,8,3072]{3,0,1,2:T(8,128)(2,1)S(1)} %copy.33, bf16[16,4,8,3072]{3,0,1,2:T(8,128)(2,1)S(1)} %copy.33, bf16[16,4,8,3072]{3,0,1,2:T(8,128)(2,1)S(1)} %copy.33, ...), branch_computations={%region_21.22_spmd, %region_22.23_spmd, %region_23.24_spmd, %regio... | conditional | bytes 9830450 | solution.py:233
  107.7 0.1 slice_bitcast_fusion.19
  107.7 1.0 collective-permute-start.26
  108.7 16.4 %collective-permute-done.26 = bf16[2,4,16,3072]{3,2,1,0:T(8,128)(2,1)S(1)} collective-permute-done((bf16[2,4,16,3072]{3,2,1,0:T(8,128)(2,1)S(1)}, bf16[2,4,16,3072]{3,2,1,0:T(8,128)(2,1)S(1)}, u32[]{:S(2)}, u32[]{:S(2)}) %collective-permute-start.26) | collective-permute-done | bytes 786464 | tf_op jit(solution)/shard_map/cond/branch_5_fun/ppermute | solution.py:27
  125.1 1.3 pad.73
  126.5 3.9 %copy.43 = bf16[4,4,16,3072]{3,0,1,2:T(4,128)(2,1)} copy(bf16[4,4,16,3072]{3,2,1,0:T(8,128)(2,1)} %get-tuple-element.246) | data formatting | bytes 3145728 | tf_op jit(solution)/shard_map/cond | solution.py:233
  132.3 3.9 %maximum_select_fusion.1 = bf16[16,4,8,3072]{3,2,1,0:T(8,128)(2,1)S(1)} fusion(bf16[16,4,8,3072]{3,2,1,0:T(8,128)(2,1)S(1)} %copy-done.8, bf16[16,4,4,3072]{3,2,1,0:T(4,128)(2,1)} %bitcast.89, pred[8]{0:T(512)(128)(4,1)S(1)} %compare_and_fusion.1), kind=kLoop, calls=%fused_computation.52 | loop fusion | flops 7864320 | bytes 7864328 | tf_op jit(solution)/shard_map/jit(_where)/select_n | solution.py:249
  136.2 1.6 slice_bitcast_fusion.21
  137.8 0.9 slice_bitcast_fusion.22
  138.7 80.5 %psum.7 = f32[16,384]{1,0:T(8,128)S(1)} all-reduce(f32[16,384]{1,0:T(8,128)S(1)} %copy-done.11), channel_id=1, replica_groups=mesh['row_0'=8,'row_1'=2,'row_2'=2,'col_0'=4,'col_1'=2] {'row_0','row_1'..., use_global_device_ids=true, to_apply=%region_28.29 | all-reduce | flops 6144 | bytes 49152 | tf_op jit(solution)/shard_map/psum | solution.py:269
  219.2 0.1 rev.9
  219.3 0.1 reshape.15
  219.5 0.8 copy.41
  220.3 0.6 slice.171
  (17 shorter events, 0.1 us)
Async XLA Ops:
  6.6 11.8 %collective-permute-start.4 = (bf16[3,4,8,3072]{3,2,1,0:T(8,128)(2,1)S(1)}, bf16[3,4,8,3072]{3,2,1,0:T(8,128)(2,1)S(1)}, u32[]{:S(2)}, u32[]{:S(2)}) collective-permute-start(bf16[3,4,8,3072]{3,2,1,0:T(8,128)(2,1)S(1)} %pad_maximum_fusion.4), channel_id=1, source_target_pairs={{0,8},{8,16},{16,24},{24,32},{32,40},{40,48},{48,56},{56,64},{64,7... | collective-permute-start | bytes 1769480 | tf_op jit(solution)/shard_map/cond/branch_4_fun/ppermute | solution.py:27
  23.9 45.9 %copy-start.12 = (s32[2]{0:T(128)S(1)}, s32[2]{0:T(128)}, u32[]{:S(2)}) copy-start(s32[2]{0:T(128)} %param.38) | copy-start | bytes 28
  23.9 46.5 %copy-start.10 = (f32[24,15,15]{0,2,1:T(8,128)S(1)}, f32[24,15,15]{0,2,1:T(8,128)}, u32[]{:S(2)}) copy-start(f32[24,15,15]{0,2,1:T(8,128)} %param.37) | copy-start | bytes 64804
  34.7 1.9 copy-start.5
  38.5 19.9 %collective-permute-start.12 = (bf16[2,4,16,3072]{3,2,1,0:T(8,128)(2,1)S(1)}, bf16[2,4,16,3072]{3,2,1,0:T(8,128)(2,1)S(1)}, u32[]{:S(2)}, u32[]{:S(2)}) collective-permute-start(bf16[2,4,16,3072]{3,2,1,0:T(8,128)(2,1)S(1)} %fusion.5), channel_id=1, source_target_pairs={{0,1},{1,2},{2,3},{3,4},{4,5},{5,6},{6,7},{7,0},{8,9},{9,10},{10,1... | collective-permute-start | bytes 2359304 | tf_op jit(solution)/shard_map/cond/branch_5_fun/ppermute | solution.py:27
  69.8 1.8 copy-start.9
  94.8 7.5 %collective-permute-start.18 = (bf16[3,4,8,3072]{3,2,1,0:T(8,128)(2,1)S(1)}, bf16[3,4,8,3072]{3,2,1,0:T(8,128)(2,1)S(1)}, u32[]{:S(2)}, u32[]{:S(2)}) collective-permute-start(bf16[3,4,8,3072]{3,2,1,0:T(8,128)(2,1)S(1)} %pad_maximum_fusion.11), channel_id=1, source_target_pairs={{0,248},{8,0},{16,8},{24,16},{32,24},{40,32},{48,40},{56,48},{64,5... | collective-permute-start | bytes 1769480 | tf_op jit(solution)/shard_map/cond/branch_4_fun/ppermute | solution.py:27
  105.7 1.7 copy-start.7
  107.7 17.4 %collective-permute-start.26 = (bf16[2,4,16,3072]{3,2,1,0:T(8,128)(2,1)S(1)}, bf16[2,4,16,3072]{3,2,1,0:T(8,128)(2,1)S(1)}, u32[]{:S(2)}, u32[]{:S(2)}) collective-permute-start(bf16[2,4,16,3072]{3,2,1,0:T(8,128)(2,1)S(1)} %slice_bitcast_fusion.19), channel_id=1, source_target_pairs={{0,7},{1,0},{2,1},{3,2},{4,3},{5,4},{6,5},{7,6},{8,15},{9,8},{10,9... | collective-permute-start | bytes 2359304 | tf_op jit(solution)/shard_map/cond/branch_5_fun/ppermute | solution.py:27
  126.5 5.9 %copy-start.8 = (bf16[16,4,8,3072]{3,2,1,0:T(8,128)(2,1)S(1)}, bf16[16,4,8,3072]{3,2,1,0:T(8,128)(2,1)}, u32[]{:S(2)}) copy-start(bf16[16,4,8,3072]{3,2,1,0:T(8,128)(2,1)} %copy-done.7) | copy-start | bytes 9437188
  136.2 2.5 %copy-start.11 = (f32[16,384]{1,0:T(8,128)S(1)}, f32[16,384]{1,0:T(8,128)}, u32[]{:S(2)}) copy-start(f32[16,384]{1,0:T(8,128)} %get-tuple-element.209) | copy-start | bytes 73732

commit v2 on v1

v2 whole, which is shorter than its diff:
```python
import functools
import math

import jax
import jax.numpy as jnp
from jax import lax
from jax.experimental import pallas as pl
from jax.experimental.pallas import tpu as pltpu
from jax.sharding import Mesh
from jax.sharding import PartitionSpec as P

ROW = ("row_0", "row_1", "row_2")
COL = ("col_0", "col_1")
ROW_COL = ("row_0", "row_1", "row_2", "col_0", "col_1")

EPSILON = 1e-06
NEG_FILL = -1e30
WIN = 8
HALF = 4
HD = 128
WINDOW_HEADS = 6
MOVE_HEADS = 12


def shifted(value, axis, steps):
    count = lax.axis_size(axis)
    pairs = [(source, (source + steps) % count) for source in range(count)]
    return lax.ppermute(value, axis, pairs)


def pulled(slot, shift, extent):
    low = jnp.where(shift <= HALF, 0, shift + extent - WIN)
    return (slot >= low) & (slot < jnp.where(shift <= HALF, shift, extent))


def head_norm(values, gain_vec):
    centred = values - jnp.mean(values, axis=-1, keepdims=True)
    variance = jnp.mean(centred * centred, axis=-1, keepdims=True)
    inv_sigma = lax.rsqrt(variance + EPSILON)
    x_hat = centred * inv_sigma
    return x_hat, inv_sigma, (x_hat * gain_vec).astype(jnp.bfloat16)


def norm_back(x_hat, inv_sigma, d_hat):
    first_mean = jnp.mean(d_hat, axis=-1, keepdims=True)
    second_mean = jnp.mean(d_hat * x_hat, axis=-1, keepdims=True)
    return inv_sigma * (d_hat - first_mean - x_hat * second_mean)


def fold_rows(values):
    return functools.reduce(jnp.add, [values[i * 8 : i * 8 + 8] for i in range(values.shape[0] // 8)])


def matmul(left, right, left_dim, right_dim, **kwargs):
    return lax.dot_general(
        left, right, (((left_dim,), (right_dim,)), ((), ())), preferred_element_type=jnp.float32, **kwargs
    )


def split(index, size):
    return index // size, index % size


def iotas(rows, cols):
    return (lax.broadcasted_iota(jnp.int32, (rows, cols), 0), lax.broadcasted_iota(jnp.int32, (rows, cols), 1))


def one_hot(condition):
    return jnp.where(condition, 1.0, 0.0).astype(jnp.bfloat16)


def strip_of_slots(spec, rows, cols):
    place, slot = iotas(rows, cols)
    (col, row), (slot_row, slot_col) = split(place, 16), split(slot, 8)
    return (row == slot_row) & (col + jnp.where(spec[1] <= HALF, 0, HALF) == slot_col)


def slots_of_strip(spec, rows, cols):
    slot, place = iotas(rows, cols)
    (col, row), (slot_row, slot_col) = split(place, 16), split(slot, 8)
    taken = (row == slot_row) & (col + jnp.where(spec[1] <= HALF, 0, HALF) == slot_col)
    return taken & pulled(slot_col, spec[1], WIN)


def row_slot(spec, place):
    row, col = split(place, 8)
    return row + jnp.where(spec[0] <= HALF, 0, 12), col


def tile_of(own_qkv, own_att, part, lanes):
    own = own_qkv[:, part, :, lanes] if part < 3 else own_att[:, :, lanes]
    return own.astype(jnp.float32).reshape(128, HD)


def row_strip_of(rows, part, lanes):
    return rows[:, part, :, lanes].astype(jnp.float32).reshape(32, HD).astype(jnp.bfloat16)


def put_tile(dqkv, att, part, lanes, result):
    rows = result.reshape(16, 8, HD).astype(jnp.bfloat16)
    if part < 3:
        dqkv[:, part, :, lanes] = rows
    else:
        att[:, :, lanes] = rows


def put_strip(strip, part, lanes, result):
    strip[:, part, :, lanes] = result.astype(jnp.bfloat16).reshape(HALF, 16, HD)


def each_part():
    return [(part, slice(head * HD, head * HD + HD)) for head in range(MOVE_HEADS) for part in range(4)]


def pack_kernel(spec, qkv, cot, hrow, strip, own_pick, row_pick):
    @pl.when(pl.program_id(0) == 0)
    def _():
        _, slot = iotas(64, 128)
        own_pick[...] = one_hot(strip_of_slots(spec, 64, 128) & ~pulled(slot // 8, spec[0], 16))
        place, source = iotas(64, 32)
        row, col = row_slot(spec, source)
        place_col, place_row = split(place, 16)
        same = (place_row == row) & (place_col + jnp.where(spec[1] <= HALF, 0, HALF) == col)
        row_pick[...] = one_hot(same & pulled(row, spec[0], 16))

    for part, lanes in each_part():
        own = tile_of(qkv, cot, part, lanes).astype(jnp.bfloat16)
        rows = row_strip_of(hrow, part, lanes)
        put_strip(strip, part, lanes, matmul(own_pick[...], own, 1, 0) + matmul(row_pick[...], rows, 1, 0))


def rows_kernel(spec, own_qkv, own_att, strip, rows, pick):
    @pl.when(pl.program_id(0) == 0)
    def _():
        slot, place = iotas(32, 64)
        row, slot_col = row_slot(spec, slot)
        col, place_row = split(place, 16)
        pick[...] = one_hot((row == place_row) & (col + jnp.where(spec[1] <= HALF, 0, HALF) == slot_col))

    slot, _ = iotas(32, HD)
    taken = pulled(slot % 8, spec[1], WIN)
    for part, lanes in each_part():
        own = own_qkv[:, part, :, lanes] if part < 3 else own_att[:, :, lanes]
        moved = matmul(pick[...], strip[:, part, :, lanes].reshape(64, HD), 1, 0)
        merged = jnp.where(taken, moved, own.astype(jnp.float32).reshape(32, HD))
        rows[:, part, :, lanes] = merged.reshape(HALF, 8, HD).astype(jnp.bfloat16)


def merge_kernel(spec, own_qkv, own_att, strip, rows, dqkv, att, pick):
    @pl.when(pl.program_id(0) == 0)
    def _():
        slot, place = iotas(128, 32)
        row, col = row_slot(spec, place)
        slot_row, slot_col = split(slot, 8)
        by_row = (slot_row == row) & (slot_col == col) & pulled(row, spec[0], 16)
        slot, _ = iotas(128, 64)
        by_col = slots_of_strip(spec, 128, 64) & ~pulled(slot // 8, spec[0], 16)
        pick[...] = jnp.concatenate([one_hot(by_col), one_hot(by_row)], axis=1)

    slot, _ = iotas(128, HD)
    taken = pulled(slot % 8, spec[1], WIN) | pulled(slot // 8, spec[0], 16)
    for part, lanes in each_part():
        back = jnp.concatenate([strip[:, part, :, lanes].reshape(64, HD), row_strip_of(rows, part, lanes)], axis=0)
        moved = matmul(pick[...], back, 1, 0)
        put_tile(dqkv, att, part, lanes, jnp.where(taken, moved, tile_of(own_qkv, own_att, part, lanes)))


def window_kernel(
    spec, qkv, cot, hcol, hrow, table, gains, labels, att, dqkv, strip, sums, mask, table_grad, gain_grad, pick, send_pick
):
    step = pl.program_id(0)
    steps = pl.num_programs(0)
    shift_row, shift_col, grid_row, grid_col = spec[0], spec[1], spec[2], spec[3]
    tokens = 128
    col_place = lambda col: (col - shift_col) & 7
    score_scale = 1.0 / math.sqrt(HD)

    @pl.when(step == 0)
    def _():
        cols = labels.shape[0]
        rows = labels.shape[1]
        col_turn = jnp.where(shift_col <= HALF, WIN, cols - WIN)
        row_turn = jnp.where(shift_row <= HALF, 16, rows - 16)
        lane = lax.broadcasted_iota(jnp.int32, (8, 128), 1)
        sub = lax.broadcasted_iota(jnp.int32, (8, 128), 0)

        def labels_at(first_row):
            base = pl.multiple_of((first_row // 128) * 128, 128)
            here = labels[pl.ds(pl.multiple_of(grid_col, 8), 8), pl.ds(base, 128)]
            there = labels[pl.ds(pl.multiple_of((grid_col + col_turn) % cols, 8), 8), pl.ds(base, 128)]
            both = jnp.where(pulled(sub, shift_col, WIN), there, here).astype(jnp.float32)
            return pltpu.roll(both, (128 - first_row % 128) % 128, 1)

        slots = jnp.where(
            pulled(lane, shift_row, 16), labels_at((grid_row + row_turn) % rows), labels_at(grid_row)
        )
        across = jnp.concatenate([jnp.broadcast_to(slots[:, i : i + 1], (8, 128)) for i in range(16)], axis=0)
        query = lax.broadcasted_iota(jnp.int32, (tokens, tokens), 0) // 8
        key = lax.broadcasted_iota(jnp.int32, (tokens, tokens), 1) // 8
        same = (((query - shift_row) & 15) // 8) == (((key - shift_row) & 15) // 8)
        mask[...] = jnp.where(same & (across == across.T), 0.0, NEG_FILL)
        gain_grad[...] = jnp.zeros_like(gain_grad)
        slot, place = iotas(tokens, 32)
        row, col = row_slot(spec, place)
        slot_row, slot_col = split(slot, 8)
        by_row = (slot_row == row) & (slot_col == col) & pulled(row, shift_row, 16)
        by_row = one_hot(by_row & ~pulled(slot_col, shift_col, WIN))
        pick[...] = jnp.concatenate([one_hot(slots_of_strip(spec, tokens, 64)), by_row], axis=1)
        send_pick[...] = one_hot(strip_of_slots(spec, 64, tokens))

    slot, _ = iotas(tokens, HD)
    taken = pulled(slot % 8, shift_col, WIN) | pulled(slot // 8, shift_row, 16)

    def load(head, part):
        lanes = slice(head * HD, head * HD + HD)
        moved = jnp.concatenate(
            [hcol[:, part, :, lanes].reshape(64, HD), row_strip_of(hrow, part, lanes)], axis=0
        )
        return jnp.where(taken, matmul(pick[...], moved, 1, 0), tile_of(qkv, cot, part, lanes))

    def put(head, part, result):
        lanes = slice(head * HD, head * HD + HD)
        put_tile(dqkv, att, part, lanes, result)
        put_strip(strip, part, lanes, matmul(send_pick[...], result.astype(jnp.bfloat16), 1, 0))

    sub = lax.broadcasted_iota(jnp.int32, (8, 128), 0)
    lane = lax.broadcasted_iota(jnp.int32, (8, 128), 1)
    col_code = col_place(sub) - col_place(lane & 7) + WIN - 1
    gain_q = gains[0:1, :]
    gain_k = gains[1:2, :]

    heads = range(WINDOW_HEADS)

    queries = [head_norm(load(head, 0), gain_q) for head in heads]
    keys = [head_norm(load(head, 1), gain_k) for head in heads]
    values = [load(head, 2).astype(jnp.bfloat16) for head in heads]
    grads = [load(head, 3).astype(jnp.bfloat16) for head in heads]

    def bias(head):
        diagonal = jnp.zeros((8, 128), jnp.float32)
        for y in range(15):
            diagonal = jnp.where(col_code == y, table[head, y : y + 1, :], diagonal)
        return jnp.concatenate([pltpu.roll(diagonal, (row * 8 - 56) % 128, 1) for row in range(16)], axis=0)

    scores = [
        matmul(queries[head][2], keys[head][2], 1, 1) * score_scale + bias(head) + mask[...] for head in heads
    ]
    d_probs = [matmul(grads[head], values[head], 1, 1) for head in heads]
    tops = [jnp.max(scores[head], axis=-1, keepdims=True) for head in heads]
    weights = [jnp.exp(scores[head] - tops[head]) for head in heads]
    inverses = [1.0 / jnp.sum(weights[head], axis=-1, keepdims=True) for head in heads]
    row_dots = [jnp.sum(weights[head] * d_probs[head], axis=-1, keepdims=True) for head in heads]
    probs = [weights[head] * inverses[head] for head in heads]
    d_scores = [probs[head] * (d_probs[head] - row_dots[head] * inverses[head]) for head in heads]
    probs_b = [probs[head].astype(jnp.bfloat16) for head in heads]
    d_scores_b = [d_scores[head].astype(jnp.bfloat16) for head in heads]
    for head in heads:
        put(head, 3, matmul(probs_b[head], values[head], 1, 0))
        put(head, 2, matmul(probs_b[head], grads[head], 0, 0))
    d_qnorms = [matmul(d_scores_b[head], keys[head][2], 1, 0) for head in heads]
    d_knorms = [matmul(d_scores_b[head], queries[head][2], 0, 0) for head in heads]
    for head in heads:
        folded = functools.reduce(
            jnp.add,
            [pltpu.roll(d_scores[head][row * 8 : row * 8 + 8], (56 - row * 8) % 128, 1) for row in range(16)],
        )
        by_code = [jnp.sum(jnp.where(col_code == y, folded, 0.0), axis=0, keepdims=True) for y in range(15)]
        table_grad[pl.ds(pl.multiple_of((step * WINDOW_HEADS + head) * 16, 16), 16), :] = jnp.concatenate(
            by_code + [jnp.zeros((1, 128), jnp.float32)], axis=0
        )
    gain_grad[0] += functools.reduce(jnp.add, [fold_rows(d_qnorms[head] * queries[head][0]) for head in heads])
    gain_grad[1] += functools.reduce(jnp.add, [fold_rows(d_knorms[head] * keys[head][0]) for head in heads])
    for head in heads:
        put(head, 0, norm_back(queries[head][0], queries[head][1], d_qnorms[head] * (gain_q * score_scale)))
        put(head, 1, norm_back(keys[head][0], keys[head][1], d_knorms[head] * (gain_k * score_scale)))

    @pl.when(step == steps - 1)
    def _():
        group = lax.broadcasted_iota(jnp.int32, (16, 128), 0)
        member = lax.broadcasted_iota(jnp.int32, (16, 128), 1) // 8
        pick = jnp.where((group == member) & (group < 15), 1.0, 0.0)
        by_offset = matmul(pick, table_grad[...], 1, 1, precision=lax.Precision.HIGHEST)
        gain_q_sum = jnp.sum(gain_grad[0], axis=0, keepdims=True) * score_scale
        gain_k_sum = jnp.sum(gain_grad[1], axis=0, keepdims=True) * score_scale
        last = jnp.concatenate([gain_q_sum, gain_k_sum, jnp.zeros_like(gain_k_sum)], axis=1)
        is_last = lax.broadcasted_iota(jnp.int32, by_offset.shape, 0) == 15
        sums[...] = jnp.where(is_last, last, by_offset)


def qkv_spec(heads):
    return pl.BlockSpec((16, 3, 8, heads * HD), lambda i, s: (0, 0, 0, i))


def cot_spec(heads):
    return pl.BlockSpec((16, 8, heads * HD), lambda i, s: (0, 0, i))


def strip_spec(heads):
    return pl.BlockSpec((HALF, 4, 16, heads * HD), lambda i, s: (0, 0, 0, i))


def rows_spec(heads):
    return pl.BlockSpec((HALF, 4, 8, heads * HD), lambda i, s: (0, 0, 0, i))


def PICK(rows, cols):
    return pltpu.VMEM((rows, cols), jnp.bfloat16)


def bf16(*dims):
    return jax.ShapeDtypeStruct(dims, jnp.bfloat16)


def call(kernel, grid, in_specs, out_specs, out_shape, scratch, name, **kwargs):
    return pl.pallas_call(
        kernel,
        grid_spec=pltpu.PrefetchScalarGridSpec(
            num_scalar_prefetch=1, grid=grid, in_specs=in_specs, out_specs=out_specs, scratch_shapes=scratch
        ),
        out_shape=out_shape,
        compiler_params=pltpu.CompilerParams(dimension_semantics=("arbitrary",) * len(grid)),
        name=name,
        **kwargs,
    )


def pack_cols(spec, qkv, cot, hrow):
    width = cot.shape[2]
    n = MOVE_HEADS
    return call(
        pack_kernel,
        (width // (n * HD),),
        [qkv_spec(n), cot_spec(n), rows_spec(n)],
        strip_spec(n),
        bf16(HALF, 4, 16, width),
        [PICK(64, 128), PICK(64, 32)],
        "pack",
    )(spec, qkv, cot, hrow)


def pack_rows(spec, dqkv, att, strip):
    width = att.shape[2]
    n = MOVE_HEADS
    block = lambda s: jnp.where(s[0] <= HALF, 0, 3)
    return call(
        rows_kernel,
        (width // (n * HD),),
        [
            pl.BlockSpec((HALF, 3, 8, n * HD), lambda i, s: (block(s), 0, 0, i)),
            pl.BlockSpec((HALF, 8, n * HD), lambda i, s: (block(s), 0, i)),
            strip_spec(n),
        ],
        rows_spec(n),
        bf16(HALF, 4, 8, width),
        [PICK(32, 64)],
        "rows",
    )(spec, dqkv, att, strip)


def merge(spec, dqkv, att, strip, rows):
    width = att.shape[2]
    n = MOVE_HEADS
    return call(
        merge_kernel,
        (width // (n * HD),),
        [qkv_spec(n), cot_spec(n), strip_spec(n), rows_spec(n)],
        [qkv_spec(n), cot_spec(n)],
        [bf16(*dqkv.shape), bf16(*att.shape)],
        [PICK(128, 96)],
        "merge",
        cost_estimate=pl.CostEstimate(flops=2 * 10**9, transcendentals=0, bytes_accessed=9 * 10**6),
    )(spec, dqkv, att, strip, rows)


def run_windows(spec, qkv, cot, hcol, hrow, table, gains, labels):
    head_count = table.shape[0]
    n = WINDOW_HEADS
    return call(
        window_kernel,
        (head_count // n,),
        [
            qkv_spec(n),
            cot_spec(n),
            strip_spec(n),
            rows_spec(n),
            pl.BlockSpec((n, 16, 128), lambda i, s: (i, 0, 0)),
            pl.BlockSpec((2, 128), lambda i, s: (0, 0)),
            pl.BlockSpec(labels.shape, lambda i, s: (0, 0)),
        ],
        [cot_spec(n), qkv_spec(n), strip_spec(n), pl.BlockSpec((16, head_count * 16), lambda i, s: (0, 0))],
        [
            bf16(*cot.shape),
            bf16(*qkv.shape),
            bf16(*hcol.shape),
            jax.ShapeDtypeStruct((16, head_count * 16), jnp.float32),
        ],
        [
            pltpu.VMEM((128, 128), jnp.float32),
            pltpu.VMEM((head_count * 16, 128), jnp.float32),
            pltpu.VMEM((2, 8, 128), jnp.float32),
            PICK(128, 96),
            PICK(64, 128),
        ],
        "windows",
    )(spec, qkv, cot, hcol, hrow, table, gains, labels)


def spread(received, low):
    first = low % HALF
    spare = (first, HALF - first - received.shape[0], 0)
    return lax.pad(received, jnp.zeros((), received.dtype), (spare,) + ((0, 0, 0),) * (received.ndim - 1))


def by_case(shift, branch):
    case = (shift > 2).astype(jnp.int32) + (shift > HALF) + (shift > 5)
    return lax.switch(case, [branch(0, 2, -1), branch(0, 4, -1), branch(1, 4, 1), branch(2, 4, 1)])


def pull_rows(shift, pieces, beside):
    def branch(first, last, steps):
        turn = 0 if steps < 0 else 12
        return lambda: (spread(shifted(pieces(first + turn, last + turn), ROW, steps), first), beside())

    return by_case(shift, branch)


def pull_cols(shift, packed):
    def branch(s):
        first, last, steps = (0, s, -1) if s <= HALF else (s - HALF, HALF, 1)
        return lambda: spread(shifted(packed[first:last], COL, steps), first)

    return lax.switch(shift - 1, [branch(s) for s in range(1, WIN)])


def doubled(sums, rounds):
    for axis, bit in rounds:
        sums = sums + lax.ppermute(sums, axis, [(i, i ^ bit) for i in range(lax.axis_size(axis))])
    return sums


def give_back(shift, axis, strip, sums, rounds):
    def branch(first, last, steps):
        return lambda: (spread(shifted(strip[first:last], axis, -steps), first), doubled(sums, rounds))

    return by_case(shift, branch)


def local(qkv, cotangent, norm_gains, rel_table, shifts, mask_ids):
    head_count = rel_table.shape[0]
    shift_row = shifts[0]
    shift_col = shifts[1]
    qkv_t = jnp.transpose(qkv, (0, 2, 1, 3))

    def row_pieces(low, high):
        return jnp.concatenate([qkv_t[low:high], cotangent[low:high, None]], axis=1)

    def tables():
        places = [lax.axis_index(ROW) * 16, lax.axis_index(COL) * 8]
        by_col = jnp.transpose(jnp.flip(rel_table, 1), (0, 2, 1))
        spread_out = jnp.pad(jnp.repeat(by_col, 8, axis=2), ((0, 0), (0, 1), (0, 8)))
        return jnp.stack([shift_row, shift_col] + places).astype(jnp.int32), spread_out

    hrow, (spec, table) = pull_rows(shift_row, row_pieces, tables)
    packed = pack_cols(spec, qkv_t, cotangent, hrow)
    hcol = pull_cols(shift_col, packed)
    att, dqkv, strip, sums = run_windows(spec, qkv_t, cotangent, hcol, hrow, table, norm_gains, mask_ids.T)
    strip, sums = give_back(shift_col, COL, strip, sums, (("row_0", 1), ("row_0", 2), ("row_0", 4)))
    rows = pack_rows(spec, dqkv, att, strip)
    rows, sums = give_back(shift_row, ROW, rows, sums, (("col_0", 1), ("col_0", 2)))
    dqkv, att = merge(spec, dqkv, att, strip, rows)
    sums = doubled(sums, (("row_2", 1), ("col_1", 1), ("row_1", 1)))
    d_gains = sums[15, : 2 * HD].reshape(2, HD)
    d_table = jnp.transpose(jnp.flip(sums[:15], 0).reshape(15, head_count, 16)[:, :, :15], (1, 0, 2))
    return (att, jnp.transpose(dqkv, (0, 2, 1, 3)), d_gains, d_table)


def solution(mesh):
    torus = Mesh(mesh.devices.reshape(8, 2, 2, 4, 2), ROW_COL)
    placed = (P(ROW, COL, None, None), P(ROW, COL, None), P(), P(), P(), P())
    return jax.shard_map(
        local,
        mesh=torus,
        in_specs=placed,
        out_specs=(P(ROW, COL, None), P(ROW, COL, None, None), P(), P()),
        check_vma=False,
    )
```

time: 221 us -> 106 us (0.48)
  blocking collectives: 80.5 us -> 0 us
  loops' own time: 21.2 us -> 0.26 us
  local copies, waits for them, and re-layouts: 23.5 us -> 10.7 us
  starting transfers between devices: 2.74 us -> 14.4 us
  other arithmetic: 11 us -> 2.79 us
  waiting for transfers between devices: 53.8 us -> 48.5 us
  Pallas kernels: 22.1 us -> 25 us
    psum x1 -> x0, blocking collectives: 80.5 us -> none  [local(): sums = lax.psum(sums, ROW_COL)]
    ppermute x4, waiting for transfers between devices: 53.8 us -> 26 us  [shifted(): return lax.ppermute(value, axis, pairs)]
    ppermute x0 -> x8, waiting for transfers between devices: none -> 22.5 us  [doubled(): lax.ppermute(sums, axis, [(i, i ^ bit) for i in range(lax.axis_size(axis))])]
    another operation x4, loops' own time: 21.2 us -> 0.26 us  [the longest x3 0.21 us: by_case(): lax.switch(case, [branch(0, 2, -1), branch(0, 4, -1), branch(1, 4, 1), br...]
    ppermute x0 -> x8, starting transfers between devices: none -> 11.7 us  [doubled(): lax.ppermute(sums, axis, [(i, i ^ bit) for i in range(lax.axis_size(axis))])]
    select_n x2 -> x0, other arithmetic: 6.26 us -> none  [the longest x1 3.85 us: fill_cols(): jnp.where(pulled(slot, shift_col, WIN), jnp.concatenate([turned, turned],...]
    concatenate x3 -> x1, other arithmetic: 3.9 us -> 0.04 us  [row_pieces(): return jnp.concatenate([qkv_t[low:high], cotangent[low:high, None]], axis=1)]
    another operation x3 -> x1, local copies, waits for them, and re-layouts: 3.46 us -> 0.04 us
  transfers between devices with their start and end apart: 4 -> 12, of which waited for: 4 -> 9; matrix products, arithmetic and copies ran while one was open for 0% -> 4% of each run, Pallas kernels for 0% -> 4%
where the time goes in v2:
time: 106 us; the launch traced here: 107 us
  waiting for transfers between devices  48.5 us (46%)
  Pallas kernels  25 us (24%)
  starting transfers between devices  14.4 us (14%)
  local copies, waits for them, and re-layouts  10.7 us (10%)
  between operations  5.24 us (5%)
  other arithmetic  2.79 us (3%)
    ppermute x4, waiting for transfers between devices, shifted(): return lax.ppermute(value, axis, pairs)  26 us
    ppermute x8, waiting for transfers between devices, doubled(): lax.ppermute(sums, axis, [(i, i ^ bit) for i in range(lax.axis_size(axis))])  22.5 us
    pallas_call x1, Pallas kernels, run_windows(): call(window_kernel, (head_count // n,), [qkv_spec(n), cot_spec(n), strip_...  13.4 us
    ppermute x8, starting transfers between devices, doubled(): lax.ppermute(sums, axis, [(i, i ^ bit) for i in range(lax.axis_size(axis))])  11.7 us
    pallas_call x1, Pallas kernels, merge(): call(merge_kernel, (width // (n * HD),), [qkv_spec(n), cot_spec(n), strip...  4.79 us
    pad x4, local copies, waits for them, and re-layouts, spread(): lax.pad(received, jnp.zeros((), received.dtype), (spare,) + ((0, 0, 0),)...  4.51 us
    pallas_call x1, Pallas kernels, pack_cols(): call(pack_kernel, (width // (n * HD),), [qkv_spec(n), cot_spec(n), rows_s...  4.16 us
    ppermute x4, starting transfers between devices, shifted(): return lax.ppermute(value, axis, pairs)  2.77 us
  transfers between devices with their start and end apart: 12, of which 9 were waited for; matrix products, arithmetic and copies ran while one was open for 4% of the time, Pallas kernels for 4%

profile of v2, /device:TPU:96, one launch (start us, length us, event | category | flops | bytes accessed | tf_op | source)
XLA Modules:
  0.0 106.9 jit_solution(10631155366622995215)
XLA Ops:
  0.6 1.3 %fusion = (s32[1]{0:T(128)}, s32[1]{0:T(128)}) fusion(s32[2]{0:T(128)} %param.29), kind=kLoop, calls=%fused_computation.17 | loop fusion | bytes 16 | tf_op jit(solution)/shard_map/slice | solution.py:451
  6.5 12.6 %conditional.4 = (bf16[4,4,8,3072]{3,2,1,0:T(8,128)(2,1)}, s32[4]{0:T(128)S(1)}, f32[24,16,128]{2,1,0:T(8,128)S(1)}) conditional(s32[]{:T(128)} %bitcast.20, (bf16[16,3,8,3072]{3,2,1,0:T(8,128)(2,1)}, bf16[16,8,3072]{2,1,0:T(8,128)(2,1)}, s32[1]{0:T(128)}, s32[1]{0:T(128)}, f32[24,15,15]{0,2,1:T(8,128)}) %tuple.119, ...), branch_computations={%region_0.1_spmd, %region_1.2_spmd, %region_2.3_spmd, %region_3.4_... | conditional | flops 393250 | bytes 7374036 | solution.py:416
  6.5 0.0 copy-start.4
  6.5 0.9 slice_bitcast_fusion.3
  7.5 1.0 slice.56
  8.5 0.1 collective-permute-start.38
  8.7 0.1 broadcast_bitcast_fusion.3
  8.8 0.3 copy.27
  9.1 1.4 %pad_add_fusion.3 = s32[4]{0:T(128)S(1)} fusion(s32[1]{0:T(128)} %bitcast.17, s32[1]{0:T(128)} %bitcast.16, s32[1]{0:T(128)} %get-tuple-element.109, s32[1]{0:T(128)} %get-tuple-element.108), kind=kLoop, calls=%fused_computation.15 | loop fusion | flops 12 | bytes 32 | tf_op jit(solution)/shard_map/cond/branch_3_fun/stack | solution.py:461
  10.5 7.7 %collective-permute-done.38 = bf16[2,4,8,3072]{3,2,1,0:T(8,128)(2,1)S(1)} collective-permute-done((bf16[2,4,8,3072]{3,2,1,0:T(8,128)(2,1)S(1)}, bf16[2,4,8,3072]{3,2,1,0:T(8,128)(2,1)S(1)}, u32[]{:S(2)}, u32[]{:S(2)}) %collective-permute-start.38) | collective-permute-done | bytes 393248 | tf_op jit(solution)/shard_map/cond/branch_3_fun/ppermute | solution.py:28
  18.2 0.9 pad.44
  19.1 4.2 %pack.1 = bf16[4,4,16,3072]{3,2,1,0:T(8,128)(2,1)S(1)} custom-call(s32[4]{0:T(128)S(1)} %get-tuple-element.145.spec, bf16[16,3,8,3072]{3,2,1,0:T(8,128)(2,1)} %bitcast.42, bf16[16,8,3072]{2,1,0:T(8,128)(2,1)} %cot.3, bf16[4,4,8,3072]{3,2,1,0:T(8,128)(2,1)} %get-tuple-element.146.hrow), custom_call_target="tpu_custom_call" | custom-call | tf_op jit(solution)/shard_map/pack/pallas_call | solution.py:330
  23.3 21.3 %conditional.5 = (bf16[4,4,16,3072]{3,2,1,0:T(8,128)(2,1)}) conditional(s32[]{:T(128)} %bitcast.22, bf16[4,4,16,3072]{3,2,1,0:T(8,128)(2,1)S(1)} %pack.1, bf16[4,4,16,3072]{3,2,1,0:T(8,128)(2,1)S(1)} %pack.1, bf16[4,4,16,3072]{3,2,1,0:T(8,128)(2,1)S(1)} %pack.1, bf16[4,4,16,3072]{3,2,1,0:T(8,128)(2,1)S(1)} %pack.1, ...), branch_computations={%region_4.5_spmd, %region_5.6_spmd, %region_6.7_spmd, %region_7.8_... | conditional | bytes 9830450 | solution.py:432
  23.3 0.1 slice.62
  23.4 1.6 %collective-permute-start.5 = (bf16[2,4,16,3072]{3,2,1,0:T(8,128)(2,1)S(1)}, bf16[2,4,16,3072]{3,2,1,0:T(8,128)(2,1)S(1)}, u32[]{:S(2)}, u32[]{:S(2)}) collective-permute-start(bf16[2,4,16,3072]{3,2,1,0:T(8,128)(2,1)S(1)} %slice.62), channel_id=1, source_target_pairs={{0,1},{1,2},{2,3},{3,4},{4,5},{5,6},{6,7},{7,0},{8,9},{9,10},{10,1... | collective-permute-start | bytes 2359304 | tf_op jit(solution)/shard_map/cond/branch_5_fun/ppermute | solution.py:28
  25.0 18.3 %collective-permute-done.5 = bf16[2,4,16,3072]{3,2,1,0:T(8,128)(2,1)S(1)} collective-permute-done((bf16[2,4,16,3072]{3,2,1,0:T(8,128)(2,1)S(1)}, bf16[2,4,16,3072]{3,2,1,0:T(8,128)(2,1)S(1)}, u32[]{:S(2)}, u32[]{:S(2)}) %collective-permute-start.5) | collective-permute-done | bytes 786464 | tf_op jit(solution)/shard_map/cond/branch_5_fun/ppermute | solution.py:28
  43.3 1.3 %pad.50 = bf16[4,4,16,3072]{3,2,1,0:T(8,128)(2,1)} pad(bf16[2,4,16,3072]{3,2,1,0:T(8,128)(2,1)S(1)} %collective-permute-done.5, bf16[]{:T(256)} %constant.163.clone), padding=2_0x0_0x0_0x0_0 | pad | bytes 2359298 | tf_op jit(solution)/shard_map/cond/branch_5_fun/pad | solution.py:411
  44.6 13.4 %windows.1 = (bf16[16,8,3072]{2,1,0:T(8,128)(2,1)}, bf16[16,3,8,3072]{3,2,1,0:T(8,128)(2,1)}, bf16[4,4,16,3072]{3,2,1,0:T(8,128)(2,1)S(1)}, f32[16,384]{1,0:T(8,128)S(1)}) custom-call(s32[4]{0:T(128)S(1)} %get-tuple-element.145.spec, bf16[16,3,8,3072]{3,2,1,0:T(8,128)(2,1)} %bitcast.43, bf16[16,8,3072]{2,1,0:T(8,128)(2,1)S(1)} %copy-done, ...), custom_call_target="tpu_custom_call" | custom-call | tf_op jit(solution)/shard_map/windows/pallas_call | solution.py:378
  58.0 18.7 %conditional.6 = (bf16[4,4,16,3072]{3,2,1,0:T(8,128)(2,1)}, f32[16,384]{1,0:T(8,128)S(1)}) conditional(s32[]{:T(128)} %bitcast.24, (bf16[4,4,16,3072]{3,2,1,0:T(8,128)(2,1)S(1)}, f32[16,384]{1,0:T(8,128)S(1)}) %tuple.83, (bf16[4,4,16,3072]{3,2,1,0:T(8,128)(2,1)S(1)}, f32[16,384]{1,0:T(8,128)S(1)}) %tuple.83, ...), branch_computations={%region_11.12_spmd, %region_12.13_spmd, %region_13.14_spmd, %regio... | conditional | flops 18432 | bytes 10346674 | solution.py:416
  58.0 0.1 slice.66
  58.1 1.0 collective-permute-start.19
  59.1 0.1 collective-permute-start.20
  59.2 3.7 %collective-permute-done.20 = f32[16,384]{1,0:T(8,128)S(1)} collective-permute-done((f32[16,384]{1,0:T(8,128)S(1)}, f32[16,384]{1,0:T(8,128)S(1)}, u32[]{:S(2)}, u32[]{:S(2)}) %collective-permute-start.20) | collective-permute-done | bytes 24608 | tf_op jit(solution)/shard_map/cond/branch_3_fun/ppermute | solution.py:437
  63.0 4.7 %collective-permute-done.21 = f32[16,384]{1,0:T(8,128)S(1)} collective-permute-done((f32[16,384]{1,0:T(8,128)S(1)}, f32[16,384]{1,0:T(8,128)S(1)}, u32[]{:S(2)}, u32[]{:S(2)}) %collective-permute-start.21) | collective-permute-done | bytes 24608 | tf_op jit(solution)/shard_map/cond/branch_3_fun/ppermute | solution.py:437
  67.7 4.5 %collective-permute-start.22 = (f32[16,384]{1,0:T(8,128)S(1)}, f32[16,384]{1,0:T(8,128)S(1)}, u32[]{:S(2)}, u32[]{:S(2)}) collective-permute-start(f32[16,384]{1,0:T(8,128)S(1)} %add.140), channel_id=1, source_target_pairs={{0,128},{32,160},{64,192},{96,224},{128,0},{160,32},{192,64},{224,... | collective-permute-start | bytes 73736 | tf_op jit(solution)/shard_map/cond/branch_3_fun/ppermute | solution.py:437
  72.2 3.3 %collective-permute-done.22 = f32[16,384]{1,0:T(8,128)S(1)} collective-permute-done((f32[16,384]{1,0:T(8,128)S(1)}, f32[16,384]{1,0:T(8,128)S(1)}, u32[]{:S(2)}, u32[]{:S(2)}) %collective-permute-start.22) | collective-permute-done | bytes 24608 | tf_op jit(solution)/shard_map/cond/branch_3_fun/ppermute | solution.py:437
  75.4 1.3 %pad.54 = bf16[4,4,16,3072]{3,2,1,0:T(8,128)(2,1)} pad(bf16[2,4,16,3072]{3,2,1,0:T(8,128)(2,1)S(1)} %collective-permute-done.19, bf16[]{:T(256)} %constant.167.clone), padding=2_0x0_0x0_0x0_0 | pad | bytes 2359298 | tf_op jit(solution)/shard_map/cond/branch_3_fun/pad | solution.py:411
  76.8 2.6 %rows.1 = bf16[4,4,8,3072]{3,2,1,0:T(8,128)(2,1)S(1)} custom-call(s32[4]{0:T(128)S(1)} %get-tuple-element.145.spec, bf16[16,3,8,3072]{3,2,1,0:T(8,128)(2,1)} %get-tuple-element.148.own_qkv, bf16[16,8,3072]{2,1,0:T(8,128)(2,1)} %get-tuple-element.149.own_att, bf16[4,4,16,3072]{3,2,1,0:T(8,128)(2,1)} %get-tuple-element.152.strip), custom_call_target="tpu_custom_call" | custom-call | tf_op jit(solution)/shard_map/rows/pallas_call | solution.py:345
  79.4 10.3 %conditional.7 = (bf16[4,4,8,3072]{3,2,1,0:T(8,128)(2,1)}, f32[16,384]{1,0:T(8,128)}, f32[16,384]{1,0:T(8,128)S(1)}, f32[16,384]{1,0:T(8,128)}) conditional(s32[]{:T(128)} %bitcast.20, (bf16[4,4,8,3072]{3,2,1,0:T(8,128)(2,1)S(1)}, f32[16,384]{1,0:T(8,128)S(1)}) %tuple.84, (bf16[4,4,8,3072]{3,2,1,0:T(8,128)(2,1)S(1)}, ...), branch_computations={%region_15.16_spmd, %region_16.17_spmd, %region_17.18_spmd, %regio... | conditional | flops 6144 | bytes 5234842 | solution.py:416
  79.5 0.1 collective-permute-start.32
  79.6 0.1 collective-permute-start.33
  79.7 3.8 %collective-permute-done.33 = f32[16,384]{1,0:T(8,128)S(1)} collective-permute-done((f32[16,384]{1,0:T(8,128)S(1)}, f32[16,384]{1,0:T(8,128)S(1)}, u32[]{:S(2)}, u32[]{:S(2)}) %collective-permute-start.33) | collective-permute-done | bytes 24608 | tf_op jit(solution)/shard_map/cond/branch_3_fun/ppermute | solution.py:437
  83.5 0.6 add.151
  84.1 1.6 %collective-permute-start.34 = (f32[16,384]{1,0:T(8,128)}, f32[16,384]{1,0:T(8,128)}, u32[]{:S(2)}, u32[]{:S(2)}) collective-permute-start(f32[16,384]{1,0:T(8,128)} %add.151), channel_id=1, source_target_pairs={{0,4},{2,6},{4,0},{6,2},{1,5},{3,7},{5,1},{7,3},{8,12},{10,14},{12... | collective-permute-start | bytes 73736 | tf_op jit(solution)/shard_map/cond/branch_3_fun/ppermute | solution.py:437
  85.7 0.8 copy.74
  86.4 0.9 pad.57
  87.4 2.3 %collective-permute-done.34 = f32[16,384]{1,0:T(8,128)} collective-permute-done((f32[16,384]{1,0:T(8,128)}, f32[16,384]{1,0:T(8,128)}, u32[]{:S(2)}, u32[]{:S(2)}) %collective-permute-start.34) | collective-permute-done | bytes 24608 | tf_op jit(solution)/shard_map/cond/branch_3_fun/ppermute | solution.py:437
  89.7 0.7 add.168
  90.5 1.3 %collective-permute-start.39 = (f32[16,384]{1,0:T(8,128)S(1)}, f32[16,384]{1,0:T(8,128)S(1)}, u32[]{:S(2)}, u32[]{:S(2)}) collective-permute-start(f32[16,384]{1,0:T(8,128)S(1)} %add.168), channel_id=1, source_target_pairs={{0,8},{8,0},{1,9},{9,1},{2,10},{10,2},{3,11},{11,3},{4,12},{12,4},... | collective-permute-start | bytes 73736 | tf_op jit(solution)/shard_map/ppermute | solution.py:437
  91.8 0.8 collective-permute-done.39
  92.7 0.1 collective-permute-start.40
  92.7 3.7 %collective-permute-done.40 = f32[16,384]{1,0:T(8,128)S(1)} collective-permute-done((f32[16,384]{1,0:T(8,128)S(1)}, f32[16,384]{1,0:T(8,128)S(1)}, u32[]{:S(2)}, u32[]{:S(2)}) %collective-permute-start.40) | collective-permute-done | bytes 24608 | tf_op jit(solution)/shard_map/ppermute | solution.py:437
  96.5 4.0 %collective-permute-start.41 = (f32[16,384]{1,0:T(8,128)S(1)}, f32[16,384]{1,0:T(8,128)S(1)}, u32[]{:S(2)}, u32[]{:S(2)}) collective-permute-start(f32[16,384]{1,0:T(8,128)S(1)} %add.170), channel_id=1, source_target_pairs={{0,16},{16,0},{1,17},{17,1},{2,18},{18,2},{3,19},{19,3},{4,20},{20... | collective-permute-start | bytes 73736 | tf_op jit(solution)/shard_map/ppermute | solution.py:437
  100.5 4.8 %merge.1 = (bf16[16,3,8,3072]{3,2,1,0:T(8,128)(2,1)}, bf16[16,8,3072]{2,1,0:T(8,128)(2,1)}) custom-call(s32[4]{0:T(128)S(1)} %get-tuple-element.145.spec, bf16[16,3,8,3072]{3,2,1,0:T(8,128)(2,1)} %get-tuple-element.148.own_qkv, bf16[16,8,3072]{2,1,0:T(8,128)(2,1)} %get-tuple-element.149.own_att, bf16[4,4,16,3072]{3,2,1,0:T(8,128)(2,1)} %get-tuple-element.152.strip, ...), custom_call_target="tpu_custom_call" | custom-call | flops 2000000000 | bytes 9000000 | tf_op jit(solution)/shard_map/merge/pallas_call | solution.py:363
  105.3 0.6 slice.80
  105.9 0.1 rev.17
  105.9 0.1 reshape.50
  106.1 0.8 copy.19
  (19 shorter events, 0.2 us)
Async XLA Ops:
  6.5 2.1 %copy-start.4 = (f32[24,15,15]{0,2,1:T(8,128)S(1)}, f32[24,15,15]{0,2,1:T(8,128)}, u32[]{:S(2)}) copy-start(f32[24,15,15]{0,2,1:T(8,128)} %get-tuple-element.178) | copy-start | bytes 64804 | tf_op jit(solution)/shard_map/cond
  8.5 9.7 %collective-permute-start.38 = (bf16[2,4,8,3072]{3,2,1,0:T(8,128)(2,1)S(1)}, bf16[2,4,8,3072]{3,2,1,0:T(8,128)(2,1)S(1)}, u32[]{:S(2)}, u32[]{:S(2)}) collective-permute-start(bf16[2,4,8,3072]{3,2,1,0:T(8,128)(2,1)S(1)} %pad_maximum_fusion.3), channel_id=1, source_target_pairs={{0,8},{8,16},{16,24},{24,32},{32,40},{40,48},{48,56},{56,64},{64,7... | collective-permute-start | bytes 1179656 | tf_op jit(solution)/shard_map/cond/branch_3_fun/ppermute | solution.py:28
  23.3 21.3 %copy-start = (bf16[16,8,3072]{2,1,0:T(8,128)(2,1)S(1)}, bf16[16,8,3072]{2,1,0:T(8,128)(2,1)}, u32[]{:S(2)}) copy-start(bf16[16,8,3072]{2,1,0:T(8,128)(2,1)} %cot.3) | copy-start | bytes 2359300
  23.4 19.9 %collective-permute-start.5 = (bf16[2,4,16,3072]{3,2,1,0:T(8,128)(2,1)S(1)}, bf16[2,4,16,3072]{3,2,1,0:T(8,128)(2,1)S(1)}, u32[]{:S(2)}, u32[]{:S(2)}) collective-permute-start(bf16[2,4,16,3072]{3,2,1,0:T(8,128)(2,1)S(1)} %slice.62), channel_id=1, source_target_pairs={{0,1},{1,2},{2,3},{3,4},{4,5},{5,6},{6,7},{7,0},{8,9},{9,10},{10,1... | collective-permute-start | bytes 2359304 | tf_op jit(solution)/shard_map/cond/branch_5_fun/ppermute | solution.py:28
  58.1 17.3 %collective-permute-start.19 = (bf16[2,4,16,3072]{3,2,1,0:T(8,128)(2,1)S(1)}, bf16[2,4,16,3072]{3,2,1,0:T(8,128)(2,1)S(1)}, u32[]{:S(2)}, u32[]{:S(2)}) collective-permute-start(bf16[2,4,16,3072]{3,2,1,0:T(8,128)(2,1)S(1)} %slice.66), channel_id=1, source_target_pairs={{0,7},{1,0},{2,1},{3,2},{4,3},{5,4},{6,5},{7,6},{8,15},{9,8},{10,9... | collective-permute-start | bytes 2359304 | tf_op jit(solution)/shard_map/cond/branch_3_fun/ppermute | solution.py:28
  59.1 3.8 %collective-permute-start.20 = (f32[16,384]{1,0:T(8,128)S(1)}, f32[16,384]{1,0:T(8,128)S(1)}, u32[]{:S(2)}, u32[]{:S(2)}) collective-permute-start(f32[16,384]{1,0:T(8,128)S(1)} %get-tuple-element.118), channel_id=1, source_target_pairs={{0,32},{32,0},{64,96},{96,64},{128,160},{160,128},{192,224},{224,1... | collective-permute-start | bytes 73736 | tf_op jit(solution)/shard_map/cond/branch_3_fun/ppermute | solution.py:437
  63.0 4.7 %collective-permute-start.21 = (f32[16,384]{1,0:T(8,128)S(1)}, f32[16,384]{1,0:T(8,128)S(1)}, u32[]{:S(2)}, u32[]{:S(2)}) collective-permute-start(f32[16,384]{1,0:T(8,128)S(1)} %add.139), channel_id=1, source_target_pairs={{0,64},{32,96},{64,0},{96,32},{128,192},{160,224},{192,128},{224,1... | collective-permute-start | bytes 73736 | tf_op jit(solution)/shard_map/cond/branch_3_fun/ppermute | solution.py:437
  67.7 7.7 %collective-permute-start.22 = (f32[16,384]{1,0:T(8,128)S(1)}, f32[16,384]{1,0:T(8,128)S(1)}, u32[]{:S(2)}, u32[]{:S(2)}) collective-permute-start(f32[16,384]{1,0:T(8,128)S(1)} %add.140), channel_id=1, source_target_pairs={{0,128},{32,160},{64,192},{96,224},{128,0},{160,32},{192,64},{224,... | collective-permute-start | bytes 73736 | tf_op jit(solution)/shard_map/cond/branch_3_fun/ppermute | solution.py:437
  79.5 7.0 %collective-permute-start.32 = (bf16[2,4,8,3072]{3,2,1,0:T(8,128)(2,1)S(1)}, bf16[2,4,8,3072]{3,2,1,0:T(8,128)(2,1)S(1)}, u32[]{:S(2)}, u32[]{:S(2)}) collective-permute-start(bf16[2,4,8,3072]{3,2,1,0:T(8,128)(2,1)S(1)} %slice.69), channel_id=1, source_target_pairs={{0,248},{8,0},{16,8},{24,16},{32,24},{40,32},{48,40},{56,48},{64,5... | collective-permute-start | bytes 1179656 | tf_op jit(solution)/shard_map/cond/branch_3_fun/ppermute | solution.py:28
  79.6 3.9 %collective-permute-start.33 = (f32[16,384]{1,0:T(8,128)S(1)}, f32[16,384]{1,0:T(8,128)S(1)}, u32[]{:S(2)}, u32[]{:S(2)}) collective-permute-start(f32[16,384]{1,0:T(8,128)S(1)} %get-tuple-element.126), channel_id=1, source_target_pairs={{0,2},{2,0},{4,6},{6,4},{1,3},{3,1},{5,7},{7,5},{8,10},{10,8},{12,... | collective-permute-start | bytes 73736 | tf_op jit(solution)/shard_map/cond/branch_3_fun/ppermute | solution.py:437
  84.1 5.6 %collective-permute-start.34 = (f32[16,384]{1,0:T(8,128)}, f32[16,384]{1,0:T(8,128)}, u32[]{:S(2)}, u32[]{:S(2)}) collective-permute-start(f32[16,384]{1,0:T(8,128)} %add.151), channel_id=1, source_target_pairs={{0,4},{2,6},{4,0},{6,2},{1,5},{3,7},{5,1},{7,3},{8,12},{10,14},{12... | collective-permute-start | bytes 73736 | tf_op jit(solution)/shard_map/cond/branch_3_fun/ppermute | solution.py:437
  90.5 2.2 %collective-permute-start.39 = (f32[16,384]{1,0:T(8,128)S(1)}, f32[16,384]{1,0:T(8,128)S(1)}, u32[]{:S(2)}, u32[]{:S(2)}) collective-permute-start(f32[16,384]{1,0:T(8,128)S(1)} %add.168), channel_id=1, source_target_pairs={{0,8},{8,0},{1,9},{9,1},{2,10},{10,2},{3,11},{11,3},{4,12},{12,4},... | collective-permute-start | bytes 73736 | tf_op jit(solution)/shard_map/ppermute | solution.py:437
  92.7 3.8 %collective-permute-start.40 = (f32[16,384]{1,0:T(8,128)S(1)}, f32[16,384]{1,0:T(8,128)S(1)}, u32[]{:S(2)}, u32[]{:S(2)}) collective-permute-start(f32[16,384]{1,0:T(8,128)S(1)} %add.169), channel_id=1, source_target_pairs={{0,1},{1,0},{2,3},{3,2},{4,5},{5,4},{6,7},{7,6},{8,9},{9,8},{10,11... | collective-permute-start | bytes 73736 | tf_op jit(solution)/shard_map/ppermute | solution.py:437
  96.5 8.8 %collective-permute-start.41 = (f32[16,384]{1,0:T(8,128)S(1)}, f32[16,384]{1,0:T(8,128)S(1)}, u32[]{:S(2)}, u32[]{:S(2)}) collective-permute-start(f32[16,384]{1,0:T(8,128)S(1)} %add.170), channel_id=1, source_target_pairs={{0,16},{16,0},{1,17},{17,1},{2,18},{18,2},{3,19},{19,3},{4,20},{20... | collective-permute-start | bytes 73736 | tf_op jit(solution)/shard_map/ppermute | solution.py:437
